TPU v7x, 32 devices: a whole 2x2x4 slice. The times are simulated.
32 devices in a mesh: dp: 2 (over x), fsdp: 16 (over z, y, core).
Axes of the slice: x: 2, y: 2, z: 4, core: 2. Of those that a mesh axis runs over, the one named last changes fastest.
Arguments:
- hidden: bfloat16 [16384, 512], P(('dp', 'fsdp')), parts along dimension 0
- targets: int32 [16384], P(('dp', 'fsdp')), parts along dimension 0
- weight: bfloat16 [32128, 512], P('fsdp')
Outputs:
- output 1: float32 [2], P('dp'), parts along dimension 0
- output 2: float32 [16384, 512], P(('dp', 'fsdp')), parts along dimension 0
- output 3: float32 [64256, 512], P(('dp', 'fsdp')), parts along dimension 0
There are 2 independent parts. A program takes and returns all parts, laid end to end along the dimension named above; an argument that names none is the same for every part.
All inputs are finite; a program needn't handle non-finite values.
Results may differ from a plain program's by a relative error of at most 0.001.
Values are sent between devices in bfloat16 or wider.
A program may use at most 1 GiB of HBM per device.

v0:
```python
import jax
import jax.numpy as jnp
from jax import lax
from jax.sharding import PartitionSpec as P


def solution(mesh):
    groups = mesh.shape["fsdp"]
    ring_pairs = [(src_idx, (src_idx + 1) % groups) for src_idx in range(groups)]
    tok_spec = P(("dp", "fsdp"), None)

    def local_head(hidden, targets, weight):
        tok_loc = hidden.shape[0]
        shard_rows = weight.shape[0]
        tokens = tok_loc * groups
        rank_id = lax.axis_index("fsdp")
        col_ids = jnp.arange(shard_rows, dtype=jnp.int32)

        def block_logits(w_blk, step_idx):
            owner_idx = (rank_id - step_idx) % groups
            logits = lax.dot_general(hidden, w_blk, (((1,), (1,)), ((), ())), preferred_element_type=jnp.float32)
            is_target = (targets - owner_idx * shard_rows)[:, None] == col_ids[None, :]
            return logits, is_target

        def fwd_update(fwd_state, w_blk, step_idx):
            run_max, run_sum, tgt_logit = fwd_state
            logits, is_target = block_logits(w_blk, step_idx)
            new_max = jnp.maximum(run_max, jnp.max(logits, axis=1))
            run_sum = run_sum * jnp.exp(run_max - new_max) + jnp.sum(jnp.exp(logits - new_max[:, None]), axis=1)
            tgt_logit = tgt_logit + jnp.sum(jnp.where(is_target, logits, 0.0), axis=1)
            return new_max, run_sum, tgt_logit

        def fwd_body(step_idx, loop_state):
            w_cur, fwd_state = loop_state
            w_cur = lax.ppermute(w_cur, "fsdp", ring_pairs)
            return w_cur, fwd_update(fwd_state, w_cur, step_idx)

        init_state = (jnp.full((tok_loc,), -jnp.inf, jnp.float32), jnp.zeros((tok_loc,), jnp.float32), jnp.zeros((tok_loc,), jnp.float32))
        first_state = fwd_update(init_state, weight, 0)
        run_max, run_sum, tgt_logit = lax.fori_loop(1, groups, fwd_body, (weight, first_state))[1]
        log_norm = run_max + jnp.log(run_sum)
        loss_val = lax.psum(jnp.sum(log_norm - tgt_logit) / tokens, "fsdp").reshape(1)

        def bwd_update(w_blk, step_idx):
            logits, is_target = block_logits(w_blk, step_idx)
            dlogits = ((jnp.exp(logits - log_norm[:, None]) - is_target.astype(jnp.float32)) / tokens).astype(jnp.bfloat16)
            dh_part = jnp.dot(dlogits, w_blk, preferred_element_type=jnp.float32)
            dw_part = lax.dot_general(dlogits, hidden, (((0,), (0,)), ((), ())), preferred_element_type=jnp.float32)
            return dh_part, dw_part

        def bwd_body(step_idx, loop_state):
            w_cur, dw_acc, grad_h = loop_state
            w_cur = lax.ppermute(w_cur, "fsdp", ring_pairs)
            dw_acc = lax.ppermute(dw_acc, "fsdp", ring_pairs)
            dh_part, dw_part = bwd_update(w_cur, step_idx)
            return w_cur, dw_acc + dw_part, grad_h + dh_part

        grad_h, dw_acc = bwd_update(weight, 0)
        final_state = lax.fori_loop(1, groups, bwd_body, (weight, dw_acc, grad_h))
        grad_w = lax.ppermute(final_state[1], "fsdp", ring_pairs)
        return loss_val, final_state[2], grad_w

    return jax.shard_map(local_head, mesh=mesh, in_specs=(tok_spec, P(("dp", "fsdp")), P("fsdp", None)), out_specs=(P("dp"), tok_spec, tok_spec), check_vma=False)
```

profile of v0, /device:TPU:0, one launch (start us, length us, event | category | flops | bytes accessed | tf_op | source)
XLA Modules:
  0.0 1800.8 jit_solution(1013063761591882174)
XLA Ops:
  10.2 473.9 %while.42 = (s32[]{:T(128)}, bf16[2008,512]{1,0:T(8,128)(2,1)}, f32[512]{0:T(512)S(1)}, f32[512]{0:T(512)S(1)}, f32[512]{0:T(512)S(1)}, /*index=5*/bf16[512,512]...) while((s32[]{:T(128)}, bf16[2008,512]{1,0:T(8,128)(2,1)}, ...), condition=%wide.region_7.8_spmd.clone, body=%wide.region_3.7_spmd.clone.sunk | while | flops 1058940416 | bytes 23183656 | solution.py:40
  10.8 28.3 %collective-permute-done = bf16[2008,512]{1,0:T(8,128)(2,1)S(1)} collective-permute-done((bf16[2008,512]{1,0:T(8,128)(2,1)}, bf16[2008,512]{1,0:T(8,128)(2,1)S(1)}, u32[]{:S(2)}, u32[]{:S(2)}) %collective-permute-start) | collective-permute-done | bytes 2056224 | tf_op jit(solution)/shard_map/while/body/eval_jaxpr/ppermute | solution.py:35
  42.9 27.7 %collective-permute-done = bf16[2008,512]{1,0:T(8,128)(2,1)S(1)} collective-permute-done((bf16[2008,512]{1,0:T(8,128)(2,1)}, bf16[2008,512]{1,0:T(8,128)(2,1)S(1)}, u32[]{:S(2)}, u32[]{:S(2)}) %collective-permute-start) | collective-permute-done | bytes 2056224 | tf_op jit(solution)/shard_map/while/body/eval_jaxpr/ppermute | solution.py:35
  74.4 27.7 %collective-permute-done = bf16[2008,512]{1,0:T(8,128)(2,1)S(1)} collective-permute-done((bf16[2008,512]{1,0:T(8,128)(2,1)}, bf16[2008,512]{1,0:T(8,128)(2,1)S(1)}, u32[]{:S(2)}, u32[]{:S(2)}) %collective-permute-start) | collective-permute-done | bytes 2056224 | tf_op jit(solution)/shard_map/while/body/eval_jaxpr/ppermute | solution.py:35
  105.9 27.7 %collective-permute-done = bf16[2008,512]{1,0:T(8,128)(2,1)S(1)} collective-permute-done((bf16[2008,512]{1,0:T(8,128)(2,1)}, bf16[2008,512]{1,0:T(8,128)(2,1)S(1)}, u32[]{:S(2)}, u32[]{:S(2)}) %collective-permute-start) | collective-permute-done | bytes 2056224 | tf_op jit(solution)/shard_map/while/body/eval_jaxpr/ppermute | solution.py:35
  137.4 27.7 %collective-permute-done = bf16[2008,512]{1,0:T(8,128)(2,1)S(1)} collective-permute-done((bf16[2008,512]{1,0:T(8,128)(2,1)}, bf16[2008,512]{1,0:T(8,128)(2,1)S(1)}, u32[]{:S(2)}, u32[]{:S(2)}) %collective-permute-start) | collective-permute-done | bytes 2056224 | tf_op jit(solution)/shard_map/while/body/eval_jaxpr/ppermute | solution.py:35
  168.9 27.7 %collective-permute-done = bf16[2008,512]{1,0:T(8,128)(2,1)S(1)} collective-permute-done((bf16[2008,512]{1,0:T(8,128)(2,1)}, bf16[2008,512]{1,0:T(8,128)(2,1)S(1)}, u32[]{:S(2)}, u32[]{:S(2)}) %collective-permute-start) | collective-permute-done | bytes 2056224 | tf_op jit(solution)/shard_map/while/body/eval_jaxpr/ppermute | solution.py:35
  200.4 27.7 %collective-permute-done = bf16[2008,512]{1,0:T(8,128)(2,1)S(1)} collective-permute-done((bf16[2008,512]{1,0:T(8,128)(2,1)}, bf16[2008,512]{1,0:T(8,128)(2,1)S(1)}, u32[]{:S(2)}, u32[]{:S(2)}) %collective-permute-start) | collective-permute-done | bytes 2056224 | tf_op jit(solution)/shard_map/while/body/eval_jaxpr/ppermute | solution.py:35
  232.0 27.7 %collective-permute-done = bf16[2008,512]{1,0:T(8,128)(2,1)S(1)} collective-permute-done((bf16[2008,512]{1,0:T(8,128)(2,1)}, bf16[2008,512]{1,0:T(8,128)(2,1)S(1)}, u32[]{:S(2)}, u32[]{:S(2)}) %collective-permute-start) | collective-permute-done | bytes 2056224 | tf_op jit(solution)/shard_map/while/body/eval_jaxpr/ppermute | solution.py:35
  263.5 27.7 %collective-permute-done = bf16[2008,512]{1,0:T(8,128)(2,1)S(1)} collective-permute-done((bf16[2008,512]{1,0:T(8,128)(2,1)}, bf16[2008,512]{1,0:T(8,128)(2,1)S(1)}, u32[]{:S(2)}, u32[]{:S(2)}) %collective-permute-start) | collective-permute-done | bytes 2056224 | tf_op jit(solution)/shard_map/while/body/eval_jaxpr/ppermute | solution.py:35
  295.0 27.7 %collective-permute-done = bf16[2008,512]{1,0:T(8,128)(2,1)S(1)} collective-permute-done((bf16[2008,512]{1,0:T(8,128)(2,1)}, bf16[2008,512]{1,0:T(8,128)(2,1)S(1)}, u32[]{:S(2)}, u32[]{:S(2)}) %collective-permute-start) | collective-permute-done | bytes 2056224 | tf_op jit(solution)/shard_map/while/body/eval_jaxpr/ppermute | solution.py:35
  326.5 27.7 %collective-permute-done = bf16[2008,512]{1,0:T(8,128)(2,1)S(1)} collective-permute-done((bf16[2008,512]{1,0:T(8,128)(2,1)}, bf16[2008,512]{1,0:T(8,128)(2,1)S(1)}, u32[]{:S(2)}, u32[]{:S(2)}) %collective-permute-start) | collective-permute-done | bytes 2056224 | tf_op jit(solution)/shard_map/while/body/eval_jaxpr/ppermute | solution.py:35
  358.1 27.7 %collective-permute-done = bf16[2008,512]{1,0:T(8,128)(2,1)S(1)} collective-permute-done((bf16[2008,512]{1,0:T(8,128)(2,1)}, bf16[2008,512]{1,0:T(8,128)(2,1)S(1)}, u32[]{:S(2)}, u32[]{:S(2)}) %collective-permute-start) | collective-permute-done | bytes 2056224 | tf_op jit(solution)/shard_map/while/body/eval_jaxpr/ppermute | solution.py:35
  389.6 27.7 %collective-permute-done = bf16[2008,512]{1,0:T(8,128)(2,1)S(1)} collective-permute-done((bf16[2008,512]{1,0:T(8,128)(2,1)}, bf16[2008,512]{1,0:T(8,128)(2,1)S(1)}, u32[]{:S(2)}, u32[]{:S(2)}) %collective-permute-start) | collective-permute-done | bytes 2056224 | tf_op jit(solution)/shard_map/while/body/eval_jaxpr/ppermute | solution.py:35
  421.1 27.7 %collective-permute-done = bf16[2008,512]{1,0:T(8,128)(2,1)S(1)} collective-permute-done((bf16[2008,512]{1,0:T(8,128)(2,1)}, bf16[2008,512]{1,0:T(8,128)(2,1)S(1)}, u32[]{:S(2)}, u32[]{:S(2)}) %collective-permute-start) | collective-permute-done | bytes 2056224 | tf_op jit(solution)/shard_map/while/body/eval_jaxpr/ppermute | solution.py:35
  493.5 1230.3 %while.43 = (s32[]{:T(128)}, bf16[2008,512]{1,0:T(8,128)(2,1)}, f32[2008,512]{1,0:T(8,128)}, f32[512,512]{1,0:T(8,128)}, bf16[512,512]{1,0:T(8,128)(2,1)S(1)}, /...) while((s32[]{:T(128)}, bf16[2008,512]{1,0:T(8,128)(2,1)}, ...), condition=%wide.region_11.12_spmd.clone, body=%wide.region_10.11_spmd.clone.sunk | while | flops 3165770240 | bytes 58835336 | solution.py:59
  493.5 71.8 %collective-permute-done.1 = bf16[2008,512]{1,0:T(8,128)(2,1)S(1)} collective-permute-done((bf16[2008,512]{1,0:T(8,128)(2,1)}, bf16[2008,512]{1,0:T(8,128)(2,1)S(1)}, u32[]{:S(2)}, u32[]{:S(2)}) %collective-permute-start.1) | collective-permute-done | bytes 2056224 | tf_op jit(solution)/shard_map/while/body/eval_jaxpr/ppermute | solution.py:53
  575.6 71.7 %collective-permute-done.1 = bf16[2008,512]{1,0:T(8,128)(2,1)S(1)} collective-permute-done((bf16[2008,512]{1,0:T(8,128)(2,1)}, bf16[2008,512]{1,0:T(8,128)(2,1)S(1)}, u32[]{:S(2)}, u32[]{:S(2)}) %collective-permute-start.1) | collective-permute-done | bytes 2056224 | tf_op jit(solution)/shard_map/while/body/eval_jaxpr/ppermute | solution.py:53
  657.6 71.7 %collective-permute-done.1 = bf16[2008,512]{1,0:T(8,128)(2,1)S(1)} collective-permute-done((bf16[2008,512]{1,0:T(8,128)(2,1)}, bf16[2008,512]{1,0:T(8,128)(2,1)S(1)}, u32[]{:S(2)}, u32[]{:S(2)}) %collective-permute-start.1) | collective-permute-done | bytes 2056224 | tf_op jit(solution)/shard_map/while/body/eval_jaxpr/ppermute | solution.py:53
  739.6 71.7 %collective-permute-done.1 = bf16[2008,512]{1,0:T(8,128)(2,1)S(1)} collective-permute-done((bf16[2008,512]{1,0:T(8,128)(2,1)}, bf16[2008,512]{1,0:T(8,128)(2,1)S(1)}, u32[]{:S(2)}, u32[]{:S(2)}) %collective-permute-start.1) | collective-permute-done | bytes 2056224 | tf_op jit(solution)/shard_map/while/body/eval_jaxpr/ppermute | solution.py:53
  821.6 71.7 %collective-permute-done.1 = bf16[2008,512]{1,0:T(8,128)(2,1)S(1)} collective-permute-done((bf16[2008,512]{1,0:T(8,128)(2,1)}, bf16[2008,512]{1,0:T(8,128)(2,1)S(1)}, u32[]{:S(2)}, u32[]{:S(2)}) %collective-permute-start.1) | collective-permute-done | bytes 2056224 | tf_op jit(solution)/shard_map/while/body/eval_jaxpr/ppermute | solution.py:53
  903.6 71.7 %collective-permute-done.1 = bf16[2008,512]{1,0:T(8,128)(2,1)S(1)} collective-permute-done((bf16[2008,512]{1,0:T(8,128)(2,1)}, bf16[2008,512]{1,0:T(8,128)(2,1)S(1)}, u32[]{:S(2)}, u32[]{:S(2)}) %collective-permute-start.1) | collective-permute-done | bytes 2056224 | tf_op jit(solution)/shard_map/while/body/eval_jaxpr/ppermute | solution.py:53
  985.6 71.7 %collective-permute-done.1 = bf16[2008,512]{1,0:T(8,128)(2,1)S(1)} collective-permute-done((bf16[2008,512]{1,0:T(8,128)(2,1)}, bf16[2008,512]{1,0:T(8,128)(2,1)S(1)}, u32[]{:S(2)}, u32[]{:S(2)}) %collective-permute-start.1) | collective-permute-done | bytes 2056224 | tf_op jit(solution)/shard_map/while/body/eval_jaxpr/ppermute | solution.py:53
  1067.7 71.7 %collective-permute-done.1 = bf16[2008,512]{1,0:T(8,128)(2,1)S(1)} collective-permute-done((bf16[2008,512]{1,0:T(8,128)(2,1)}, bf16[2008,512]{1,0:T(8,128)(2,1)S(1)}, u32[]{:S(2)}, u32[]{:S(2)}) %collective-permute-start.1) | collective-permute-done | bytes 2056224 | tf_op jit(solution)/shard_map/while/body/eval_jaxpr/ppermute | solution.py:53
  1149.7 71.7 %collective-permute-done.1 = bf16[2008,512]{1,0:T(8,128)(2,1)S(1)} collective-permute-done((bf16[2008,512]{1,0:T(8,128)(2,1)}, bf16[2008,512]{1,0:T(8,128)(2,1)S(1)}, u32[]{:S(2)}, u32[]{:S(2)}) %collective-permute-start.1) | collective-permute-done | bytes 2056224 | tf_op jit(solution)/shard_map/while/body/eval_jaxpr/ppermute | solution.py:53
  1231.7 71.7 %collective-permute-done.1 = bf16[2008,512]{1,0:T(8,128)(2,1)S(1)} collective-permute-done((bf16[2008,512]{1,0:T(8,128)(2,1)}, bf16[2008,512]{1,0:T(8,128)(2,1)S(1)}, u32[]{:S(2)}, u32[]{:S(2)}) %collective-permute-start.1) | collective-permute-done | bytes 2056224 | tf_op jit(solution)/shard_map/while/body/eval_jaxpr/ppermute | solution.py:53
  1313.7 71.7 %collective-permute-done.1 = bf16[2008,512]{1,0:T(8,128)(2,1)S(1)} collective-permute-done((bf16[2008,512]{1,0:T(8,128)(2,1)}, bf16[2008,512]{1,0:T(8,128)(2,1)S(1)}, u32[]{:S(2)}, u32[]{:S(2)}) %collective-permute-start.1) | collective-permute-done | bytes 2056224 | tf_op jit(solution)/shard_map/while/body/eval_jaxpr/ppermute | solution.py:53
  1395.7 71.7 %collective-permute-done.1 = bf16[2008,512]{1,0:T(8,128)(2,1)S(1)} collective-permute-done((bf16[2008,512]{1,0:T(8,128)(2,1)}, bf16[2008,512]{1,0:T(8,128)(2,1)S(1)}, u32[]{:S(2)}, u32[]{:S(2)}) %collective-permute-start.1) | collective-permute-done | bytes 2056224 | tf_op jit(solution)/shard_map/while/body/eval_jaxpr/ppermute | solution.py:53
  1477.7 71.7 %collective-permute-done.1 = bf16[2008,512]{1,0:T(8,128)(2,1)S(1)} collective-permute-done((bf16[2008,512]{1,0:T(8,128)(2,1)}, bf16[2008,512]{1,0:T(8,128)(2,1)S(1)}, u32[]{:S(2)}, u32[]{:S(2)}) %collective-permute-start.1) | collective-permute-done | bytes 2056224 | tf_op jit(solution)/shard_map/while/body/eval_jaxpr/ppermute | solution.py:53
  1559.8 71.7 %collective-permute-done.1 = bf16[2008,512]{1,0:T(8,128)(2,1)S(1)} collective-permute-done((bf16[2008,512]{1,0:T(8,128)(2,1)}, bf16[2008,512]{1,0:T(8,128)(2,1)S(1)}, u32[]{:S(2)}, u32[]{:S(2)}) %collective-permute-start.1) | collective-permute-done | bytes 2056224 | tf_op jit(solution)/shard_map/while/body/eval_jaxpr/ppermute | solution.py:53
  1641.8 71.8 %collective-permute-done.1 = bf16[2008,512]{1,0:T(8,128)(2,1)S(1)} collective-permute-done((bf16[2008,512]{1,0:T(8,128)(2,1)}, bf16[2008,512]{1,0:T(8,128)(2,1)S(1)}, u32[]{:S(2)}, u32[]{:S(2)}) %collective-permute-start.1) | collective-permute-done | bytes 2056224 | tf_op jit(solution)/shard_map/while/body/eval_jaxpr/ppermute | solution.py:53
  1724.5 71.7 %psum.7 = f32[1]{0:T(128)} all-reduce(f32[1]{0:T(128)} %bitcast), channel_id=1, replica_groups=mesh['dp'=2,'fsdp'=16] {'fsdp'}, use_global_device_ids=true, to_apply=%region_9.10 | all-reduce | flops 1 | bytes 8 | tf_op jit(solution)/shard_map/psum | solution.py:42
  (336 shorter events, 261.6 us)
Async XLA Ops:
  10.2 28.8 %collective-permute-start = (bf16[2008,512]{1,0:T(8,128)(2,1)}, bf16[2008,512]{1,0:T(8,128)(2,1)S(1)}, u32[]{:S(2)}, u32[]{:S(2)}) collective-permute-start(bf16[2008,512]{1,0:T(8,128)(2,1)} %get-tuple-element.651), channel_id=1, source_target_pairs={{0,1},{1,2},{2,3},{3,4},{4,5},{5,6},{6,7},{7,8},{8,9},{9,10},{10,1... | collective-permute-start | bytes 6168584 | tf_op jit(solution)/shard_map/while/body/eval_jaxpr/ppermute | solution.py:35
  493.5 76.2 %collective-permute-start.2 = (f32[2008,512]{1,0:T(8,128)}, f32[2008,512]{1,0:T(8,128)}, u32[]{:S(2)}, u32[]{:S(2)}) collective-permute-start(f32[2008,512]{1,0:T(8,128)} %get-tuple-element.691), channel_id=1, source_target_pairs={{0,1},{1,2},{2,3},{3,4},{4,5},{5,6},{6,7},{7,8},{8,9},{9,10},{10,1... | collective-permute-start | bytes 12337160 | tf_op jit(solution)/shard_map/while/body/eval_jaxpr/ppermute | solution.py:54
  493.5 71.8 %collective-permute-start.1 = (bf16[2008,512]{1,0:T(8,128)(2,1)}, bf16[2008,512]{1,0:T(8,128)(2,1)S(1)}, u32[]{:S(2)}, u32[]{:S(2)}) collective-permute-start(bf16[2008,512]{1,0:T(8,128)(2,1)} %get-tuple-element.690), channel_id=1, source_target_pairs={{0,1},{1,2},{2,3},{3,4},{4,5},{5,6},{6,7},{7,8},{8,9},{9,10},{10,1... | collective-permute-start | bytes 6168584 | tf_op jit(solution)/shard_map/while/body/eval_jaxpr/ppermute | solution.py:53
  575.5 76.3 %collective-permute-start.2 = (f32[2008,512]{1,0:T(8,128)}, f32[2008,512]{1,0:T(8,128)}, u32[]{:S(2)}, u32[]{:S(2)}) collective-permute-start(f32[2008,512]{1,0:T(8,128)} %get-tuple-element.691), channel_id=1, source_target_pairs={{0,1},{1,2},{2,3},{3,4},{4,5},{5,6},{6,7},{7,8},{8,9},{9,10},{10,1... | collective-permute-start | bytes 12337160 | tf_op jit(solution)/shard_map/while/body/eval_jaxpr/ppermute | solution.py:54
  575.5 71.8 %collective-permute-start.1 = (bf16[2008,512]{1,0:T(8,128)(2,1)}, bf16[2008,512]{1,0:T(8,128)(2,1)S(1)}, u32[]{:S(2)}, u32[]{:S(2)}) collective-permute-start(bf16[2008,512]{1,0:T(8,128)(2,1)} %get-tuple-element.690), channel_id=1, source_target_pairs={{0,1},{1,2},{2,3},{3,4},{4,5},{5,6},{6,7},{7,8},{8,9},{9,10},{10,1... | collective-permute-start | bytes 6168584 | tf_op jit(solution)/shard_map/while/body/eval_jaxpr/ppermute | solution.py:53
  657.5 76.2 %collective-permute-start.2 = (f32[2008,512]{1,0:T(8,128)}, f32[2008,512]{1,0:T(8,128)}, u32[]{:S(2)}, u32[]{:S(2)}) collective-permute-start(f32[2008,512]{1,0:T(8,128)} %get-tuple-element.691), channel_id=1, source_target_pairs={{0,1},{1,2},{2,3},{3,4},{4,5},{5,6},{6,7},{7,8},{8,9},{9,10},{10,1... | collective-permute-start | bytes 12337160 | tf_op jit(solution)/shard_map/while/body/eval_jaxpr/ppermute | solution.py:54
  657.5 71.8 %collective-permute-start.1 = (bf16[2008,512]{1,0:T(8,128)(2,1)}, bf16[2008,512]{1,0:T(8,128)(2,1)S(1)}, u32[]{:S(2)}, u32[]{:S(2)}) collective-permute-start(bf16[2008,512]{1,0:T(8,128)(2,1)} %get-tuple-element.690), channel_id=1, source_target_pairs={{0,1},{1,2},{2,3},{3,4},{4,5},{5,6},{6,7},{7,8},{8,9},{9,10},{10,1... | collective-permute-start | bytes 6168584 | tf_op jit(solution)/shard_map/while/body/eval_jaxpr/ppermute | solution.py:53
  739.6 76.3 %collective-permute-start.2 = (f32[2008,512]{1,0:T(8,128)}, f32[2008,512]{1,0:T(8,128)}, u32[]{:S(2)}, u32[]{:S(2)}) collective-permute-start(f32[2008,512]{1,0:T(8,128)} %get-tuple-element.691), channel_id=1, source_target_pairs={{0,1},{1,2},{2,3},{3,4},{4,5},{5,6},{6,7},{7,8},{8,9},{9,10},{10,1... | collective-permute-start | bytes 12337160 | tf_op jit(solution)/shard_map/while/body/eval_jaxpr/ppermute | solution.py:54
  739.6 71.8 %collective-permute-start.1 = (bf16[2008,512]{1,0:T(8,128)(2,1)}, bf16[2008,512]{1,0:T(8,128)(2,1)S(1)}, u32[]{:S(2)}, u32[]{:S(2)}) collective-permute-start(bf16[2008,512]{1,0:T(8,128)(2,1)} %get-tuple-element.690), channel_id=1, source_target_pairs={{0,1},{1,2},{2,3},{3,4},{4,5},{5,6},{6,7},{7,8},{8,9},{9,10},{10,1... | collective-permute-start | bytes 6168584 | tf_op jit(solution)/shard_map/while/body/eval_jaxpr/ppermute | solution.py:53
  821.6 76.2 %collective-permute-start.2 = (f32[2008,512]{1,0:T(8,128)}, f32[2008,512]{1,0:T(8,128)}, u32[]{:S(2)}, u32[]{:S(2)}) collective-permute-start(f32[2008,512]{1,0:T(8,128)} %get-tuple-element.691), channel_id=1, source_target_pairs={{0,1},{1,2},{2,3},{3,4},{4,5},{5,6},{6,7},{7,8},{8,9},{9,10},{10,1... | collective-permute-start | bytes 12337160 | tf_op jit(solution)/shard_map/while/body/eval_jaxpr/ppermute | solution.py:54
  821.6 71.8 %collective-permute-start.1 = (bf16[2008,512]{1,0:T(8,128)(2,1)}, bf16[2008,512]{1,0:T(8,128)(2,1)S(1)}, u32[]{:S(2)}, u32[]{:S(2)}) collective-permute-start(bf16[2008,512]{1,0:T(8,128)(2,1)} %get-tuple-element.690), channel_id=1, source_target_pairs={{0,1},{1,2},{2,3},{3,4},{4,5},{5,6},{6,7},{7,8},{8,9},{9,10},{10,1... | collective-permute-start | bytes 6168584 | tf_op jit(solution)/shard_map/while/body/eval_jaxpr/ppermute | solution.py:53
  903.6 76.3 %collective-permute-start.2 = (f32[2008,512]{1,0:T(8,128)}, f32[2008,512]{1,0:T(8,128)}, u32[]{:S(2)}, u32[]{:S(2)}) collective-permute-start(f32[2008,512]{1,0:T(8,128)} %get-tuple-element.691), channel_id=1, source_target_pairs={{0,1},{1,2},{2,3},{3,4},{4,5},{5,6},{6,7},{7,8},{8,9},{9,10},{10,1... | collective-permute-start | bytes 12337160 | tf_op jit(solution)/shard_map/while/body/eval_jaxpr/ppermute | solution.py:54
  903.6 71.8 %collective-permute-start.1 = (bf16[2008,512]{1,0:T(8,128)(2,1)}, bf16[2008,512]{1,0:T(8,128)(2,1)S(1)}, u32[]{:S(2)}, u32[]{:S(2)}) collective-permute-start(bf16[2008,512]{1,0:T(8,128)(2,1)} %get-tuple-element.690), channel_id=1, source_target_pairs={{0,1},{1,2},{2,3},{3,4},{4,5},{5,6},{6,7},{7,8},{8,9},{9,10},{10,1... | collective-permute-start | bytes 6168584 | tf_op jit(solution)/shard_map/while/body/eval_jaxpr/ppermute | solution.py:53
  985.6 76.2 %collective-permute-start.2 = (f32[2008,512]{1,0:T(8,128)}, f32[2008,512]{1,0:T(8,128)}, u32[]{:S(2)}, u32[]{:S(2)}) collective-permute-start(f32[2008,512]{1,0:T(8,128)} %get-tuple-element.691), channel_id=1, source_target_pairs={{0,1},{1,2},{2,3},{3,4},{4,5},{5,6},{6,7},{7,8},{8,9},{9,10},{10,1... | collective-permute-start | bytes 12337160 | tf_op jit(solution)/shard_map/while/body/eval_jaxpr/ppermute | solution.py:54
  985.6 71.8 %collective-permute-start.1 = (bf16[2008,512]{1,0:T(8,128)(2,1)}, bf16[2008,512]{1,0:T(8,128)(2,1)S(1)}, u32[]{:S(2)}, u32[]{:S(2)}) collective-permute-start(bf16[2008,512]{1,0:T(8,128)(2,1)} %get-tuple-element.690), channel_id=1, source_target_pairs={{0,1},{1,2},{2,3},{3,4},{4,5},{5,6},{6,7},{7,8},{8,9},{9,10},{10,1... | collective-permute-start | bytes 6168584 | tf_op jit(solution)/shard_map/while/body/eval_jaxpr/ppermute | solution.py:53
  1067.6 76.3 %collective-permute-start.2 = (f32[2008,512]{1,0:T(8,128)}, f32[2008,512]{1,0:T(8,128)}, u32[]{:S(2)}, u32[]{:S(2)}) collective-permute-start(f32[2008,512]{1,0:T(8,128)} %get-tuple-element.691), channel_id=1, source_target_pairs={{0,1},{1,2},{2,3},{3,4},{4,5},{5,6},{6,7},{7,8},{8,9},{9,10},{10,1... | collective-permute-start | bytes 12337160 | tf_op jit(solution)/shard_map/while/body/eval_jaxpr/ppermute | solution.py:54
  1067.6 71.8 %collective-permute-start.1 = (bf16[2008,512]{1,0:T(8,128)(2,1)}, bf16[2008,512]{1,0:T(8,128)(2,1)S(1)}, u32[]{:S(2)}, u32[]{:S(2)}) collective-permute-start(bf16[2008,512]{1,0:T(8,128)(2,1)} %get-tuple-element.690), channel_id=1, source_target_pairs={{0,1},{1,2},{2,3},{3,4},{4,5},{5,6},{6,7},{7,8},{8,9},{9,10},{10,1... | collective-permute-start | bytes 6168584 | tf_op jit(solution)/shard_map/while/body/eval_jaxpr/ppermute | solution.py:53
  1149.6 76.2 %collective-permute-start.2 = (f32[2008,512]{1,0:T(8,128)}, f32[2008,512]{1,0:T(8,128)}, u32[]{:S(2)}, u32[]{:S(2)}) collective-permute-start(f32[2008,512]{1,0:T(8,128)} %get-tuple-element.691), channel_id=1, source_target_pairs={{0,1},{1,2},{2,3},{3,4},{4,5},{5,6},{6,7},{7,8},{8,9},{9,10},{10,1... | collective-permute-start | bytes 12337160 | tf_op jit(solution)/shard_map/while/body/eval_jaxpr/ppermute | solution.py:54
  1149.6 71.8 %collective-permute-start.1 = (bf16[2008,512]{1,0:T(8,128)(2,1)}, bf16[2008,512]{1,0:T(8,128)(2,1)S(1)}, u32[]{:S(2)}, u32[]{:S(2)}) collective-permute-start(bf16[2008,512]{1,0:T(8,128)(2,1)} %get-tuple-element.690), channel_id=1, source_target_pairs={{0,1},{1,2},{2,3},{3,4},{4,5},{5,6},{6,7},{7,8},{8,9},{9,10},{10,1... | collective-permute-start | bytes 6168584 | tf_op jit(solution)/shard_map/while/body/eval_jaxpr/ppermute | solution.py:53
  1231.7 76.3 %collective-permute-start.2 = (f32[2008,512]{1,0:T(8,128)}, f32[2008,512]{1,0:T(8,128)}, u32[]{:S(2)}, u32[]{:S(2)}) collective-permute-start(f32[2008,512]{1,0:T(8,128)} %get-tuple-element.691), channel_id=1, source_target_pairs={{0,1},{1,2},{2,3},{3,4},{4,5},{5,6},{6,7},{7,8},{8,9},{9,10},{10,1... | collective-permute-start | bytes 12337160 | tf_op jit(solution)/shard_map/while/body/eval_jaxpr/ppermute | solution.py:54
  1231.7 71.8 %collective-permute-start.1 = (bf16[2008,512]{1,0:T(8,128)(2,1)}, bf16[2008,512]{1,0:T(8,128)(2,1)S(1)}, u32[]{:S(2)}, u32[]{:S(2)}) collective-permute-start(bf16[2008,512]{1,0:T(8,128)(2,1)} %get-tuple-element.690), channel_id=1, source_target_pairs={{0,1},{1,2},{2,3},{3,4},{4,5},{5,6},{6,7},{7,8},{8,9},{9,10},{10,1... | collective-permute-start | bytes 6168584 | tf_op jit(solution)/shard_map/while/body/eval_jaxpr/ppermute | solution.py:53
  1313.7 76.2 %collective-permute-start.2 = (f32[2008,512]{1,0:T(8,128)}, f32[2008,512]{1,0:T(8,128)}, u32[]{:S(2)}, u32[]{:S(2)}) collective-permute-start(f32[2008,512]{1,0:T(8,128)} %get-tuple-element.691), channel_id=1, source_target_pairs={{0,1},{1,2},{2,3},{3,4},{4,5},{5,6},{6,7},{7,8},{8,9},{9,10},{10,1... | collective-permute-start | bytes 12337160 | tf_op jit(solution)/shard_map/while/body/eval_jaxpr/ppermute | solution.py:54
  1313.7 71.8 %collective-permute-start.1 = (bf16[2008,512]{1,0:T(8,128)(2,1)}, bf16[2008,512]{1,0:T(8,128)(2,1)S(1)}, u32[]{:S(2)}, u32[]{:S(2)}) collective-permute-start(bf16[2008,512]{1,0:T(8,128)(2,1)} %get-tuple-element.690), channel_id=1, source_target_pairs={{0,1},{1,2},{2,3},{3,4},{4,5},{5,6},{6,7},{7,8},{8,9},{9,10},{10,1... | collective-permute-start | bytes 6168584 | tf_op jit(solution)/shard_map/while/body/eval_jaxpr/ppermute | solution.py:53
  1395.7 76.3 %collective-permute-start.2 = (f32[2008,512]{1,0:T(8,128)}, f32[2008,512]{1,0:T(8,128)}, u32[]{:S(2)}, u32[]{:S(2)}) collective-permute-start(f32[2008,512]{1,0:T(8,128)} %get-tuple-element.691), channel_id=1, source_target_pairs={{0,1},{1,2},{2,3},{3,4},{4,5},{5,6},{6,7},{7,8},{8,9},{9,10},{10,1... | collective-permute-start | bytes 12337160 | tf_op jit(solution)/shard_map/while/body/eval_jaxpr/ppermute | solution.py:54
  1395.7 71.8 %collective-permute-start.1 = (bf16[2008,512]{1,0:T(8,128)(2,1)}, bf16[2008,512]{1,0:T(8,128)(2,1)S(1)}, u32[]{:S(2)}, u32[]{:S(2)}) collective-permute-start(bf16[2008,512]{1,0:T(8,128)(2,1)} %get-tuple-element.690), channel_id=1, source_target_pairs={{0,1},{1,2},{2,3},{3,4},{4,5},{5,6},{6,7},{7,8},{8,9},{9,10},{10,1... | collective-permute-start | bytes 6168584 | tf_op jit(solution)/shard_map/while/body/eval_jaxpr/ppermute | solution.py:53
  1477.7 76.2 %collective-permute-start.2 = (f32[2008,512]{1,0:T(8,128)}, f32[2008,512]{1,0:T(8,128)}, u32[]{:S(2)}, u32[]{:S(2)}) collective-permute-start(f32[2008,512]{1,0:T(8,128)} %get-tuple-element.691), channel_id=1, source_target_pairs={{0,1},{1,2},{2,3},{3,4},{4,5},{5,6},{6,7},{7,8},{8,9},{9,10},{10,1... | collective-permute-start | bytes 12337160 | tf_op jit(solution)/shard_map/while/body/eval_jaxpr/ppermute | solution.py:54
  1477.7 71.8 %collective-permute-start.1 = (bf16[2008,512]{1,0:T(8,128)(2,1)}, bf16[2008,512]{1,0:T(8,128)(2,1)S(1)}, u32[]{:S(2)}, u32[]{:S(2)}) collective-permute-start(bf16[2008,512]{1,0:T(8,128)(2,1)} %get-tuple-element.690), channel_id=1, source_target_pairs={{0,1},{1,2},{2,3},{3,4},{4,5},{5,6},{6,7},{7,8},{8,9},{9,10},{10,1... | collective-permute-start | bytes 6168584 | tf_op jit(solution)/shard_map/while/body/eval_jaxpr/ppermute | solution.py:53
  1559.7 76.3 %collective-permute-start.2 = (f32[2008,512]{1,0:T(8,128)}, f32[2008,512]{1,0:T(8,128)}, u32[]{:S(2)}, u32[]{:S(2)}) collective-permute-start(f32[2008,512]{1,0:T(8,128)} %get-tuple-element.691), channel_id=1, source_target_pairs={{0,1},{1,2},{2,3},{3,4},{4,5},{5,6},{6,7},{7,8},{8,9},{9,10},{10,1... | collective-permute-start | bytes 12337160 | tf_op jit(solution)/shard_map/while/body/eval_jaxpr/ppermute | solution.py:54
  1559.7 71.8 %collective-permute-start.1 = (bf16[2008,512]{1,0:T(8,128)(2,1)}, bf16[2008,512]{1,0:T(8,128)(2,1)S(1)}, u32[]{:S(2)}, u32[]{:S(2)}) collective-permute-start(bf16[2008,512]{1,0:T(8,128)(2,1)} %get-tuple-element.690), channel_id=1, source_target_pairs={{0,1},{1,2},{2,3},{3,4},{4,5},{5,6},{6,7},{7,8},{8,9},{9,10},{10,1... | collective-permute-start | bytes 6168584 | tf_op jit(solution)/shard_map/while/body/eval_jaxpr/ppermute | solution.py:53
  1641.7 76.3 %collective-permute-start.2 = (f32[2008,512]{1,0:T(8,128)}, f32[2008,512]{1,0:T(8,128)}, u32[]{:S(2)}, u32[]{:S(2)}) collective-permute-start(f32[2008,512]{1,0:T(8,128)} %get-tuple-element.691), channel_id=1, source_target_pairs={{0,1},{1,2},{2,3},{3,4},{4,5},{5,6},{6,7},{7,8},{8,9},{9,10},{10,1... | collective-permute-start | bytes 12337160 | tf_op jit(solution)/shard_map/while/body/eval_jaxpr/ppermute | solution.py:54
  1641.7 71.8 %collective-permute-start.1 = (bf16[2008,512]{1,0:T(8,128)(2,1)}, bf16[2008,512]{1,0:T(8,128)(2,1)S(1)}, u32[]{:S(2)}, u32[]{:S(2)}) collective-permute-start(bf16[2008,512]{1,0:T(8,128)(2,1)} %get-tuple-element.690), channel_id=1, source_target_pairs={{0,1},{1,2},{2,3},{3,4},{4,5},{5,6},{6,7},{7,8},{8,9},{9,10},{10,1... | collective-permute-start | bytes 6168584 | tf_op jit(solution)/shard_map/while/body/eval_jaxpr/ppermute | solution.py:53
  1723.8 72.4 %collective-permute-start.3 = (f32[2008,512]{1,0:T(8,128)}, f32[2008,512]{1,0:T(8,128)}, u32[]{:S(2)}, u32[]{:S(2)}) collective-permute-start(f32[2008,512]{1,0:T(8,128)} %get-tuple-element.452), channel_id=1, source_target_pairs={{0,1},{1,2},{2,3},{3,4},{4,5},{5,6},{6,7},{7,8},{8,9},{9,10},{10,1... | collective-permute-start | bytes 12337160 | tf_op jit(solution)/shard_map/ppermute | solution.py:60
  (48 other events, 518.9 us)
where the time goes:
time: 1800 us
  waiting for transfers between devices  1490 us (83%)
  matrix products  164 us (9%)
  blocking collectives  71.7 us (4%)
  local copies, waits for them, and re-layouts  47.4 us (3%)
  other arithmetic  21.8 us (1%)
    ppermute x15, waiting for transfers between devices, bwd_body(): w_cur = lax.ppermute(w_cur, 'fsdp', ring_pairs)  1080 us
    ppermute x15, waiting for transfers between devices, fwd_body(): w_cur = lax.ppermute(w_cur, 'fsdp', ring_pairs)  416 us
    dot_general x16, matrix products, bwd_update(): lax.dot_general(dlogits, hidden, (((0,), (0,)), ((), ())), preferred_elem...  89.7 us
    psum x1, blocking collectives, local_head(): lax.psum(jnp.sum(log_norm - tgt_logit) / tokens, 'fsdp').reshape(1)  71.7 us
    dot_general x31, matrix products, block_logits(): lax.dot_general(hidden, w_blk, (((1,), (1,)), ((), ())), preferred_elemen...  49.6 us
    while x105, local copies, waits for them, and re-layouts  39.8 us
  transfers between devices with their start and end apart: 46, of which 30 were waited for; matrix products, arithmetic and copies ran while one was open for 4% of the time, Pallas kernels for 0%

commit v1 on v0

v1 whole, which is shorter than its diff:
```python
import jax
import jax.numpy as jnp
from jax import lax
from jax.sharding import PartitionSpec as P


def solution(mesh):
    groups = mesh.shape["fsdp"]
    tok_spec = P(("dp", "fsdp"), None)

    def local_head(hidden, targets, weight):
        tokens = hidden.shape[0] * groups
        rows = weight.shape[0]
        base = lax.axis_index("fsdp") * rows
        h_all = lax.all_gather(hidden, "fsdp", axis=0, tiled=True)
        t_all = lax.all_gather(targets, "fsdp", axis=0, tiled=True)
        logits = lax.dot_general(h_all, weight, (((1,), (1,)), ((), ())), preferred_element_type=jnp.float32)
        is_target = (t_all - base)[:, None] == jnp.arange(rows, dtype=jnp.int32)[None, :]
        row_max = jnp.max(logits, axis=1)
        row_sum = jnp.sum(jnp.exp(logits - row_max[:, None]), axis=1)
        tgt = jnp.sum(jnp.where(is_target, logits, 0.0), axis=1)
        stats = lax.all_gather(jnp.stack([row_max, row_sum, tgt]), "fsdp", axis=0)
        all_max = jnp.max(stats[:, 0], axis=0)
        lse = all_max + jnp.log(jnp.sum(stats[:, 1] * jnp.exp(stats[:, 0] - all_max), axis=0))
        loss = (jnp.sum(lse - jnp.sum(stats[:, 2], axis=0)) / tokens).reshape(1)
        dz = ((jnp.exp(logits - lse[:, None]) - is_target.astype(jnp.float32)) / tokens).astype(jnp.bfloat16)
        dh = jnp.dot(dz, weight, preferred_element_type=jnp.float32)
        dh = lax.psum_scatter(dh, "fsdp", scatter_dimension=0, tiled=True)
        dw = lax.dot_general(dz, h_all, (((0,), (0,)), ((), ())), preferred_element_type=jnp.float32)
        return loss, dh, dw

    return jax.shard_map(local_head, mesh=mesh, in_specs=(tok_spec, P(("dp", "fsdp")), P("fsdp", None)), out_specs=(P("dp"), tok_spec, tok_spec), check_vma=False)
```

time: 1800 us -> 399 us (0.22)
  waiting for transfers between devices: 1490 us -> 241 us
  matrix products: 164 us -> 91.1 us
  blocking collectives: 71.7 us -> 23.3 us
  local copies, waits for them, and re-layouts: 47.4 us -> 0.01 us
    ppermute x46 -> x0, waiting for transfers between devices: 1490 us -> none  [the longest x15 1080 us: bwd_body(): w_cur = lax.ppermute(w_cur, 'fsdp', ring_pairs)]
    reduce_scatter x0 -> x1, waiting for transfers between devices: none -> 144 us  [local_head(): dh = lax.psum_scatter(dh, 'fsdp', scatter_dimension=0, tiled=True)]
    all_gather x0 -> x2, waiting for transfers between devices: none -> 96.2 us  [the longest x1 56.2 us: local_head(): h_all = lax.all_gather(hidden, 'fsdp', axis=0, tiled=True)]
    dot_general x63 -> x3, matrix products: 164 us -> 91.1 us  [the longest x1 32.7 us: local_head(): dh = jnp.dot(dz, weight, preferred_element_type=jnp.float32)]
    psum x1 -> x0, blocking collectives: 71.7 us -> none  [local_head(): lax.psum(jnp.sum(log_norm - tgt_logit) / tokens, 'fsdp').reshape(1)]
    while x105 -> x0, local copies, waits for them, and re-layouts: 39.8 us -> none
    all_gather x0 -> x1, blocking collectives: none -> 23.3 us  [local_head(): t_all = lax.all_gather(targets, 'fsdp', axis=0, tiled=True)]
  transfers between devices with their start and end apart: 46 -> 3, of which waited for: 30 -> 3; matrix products, arithmetic and copies ran while one was open for 4% -> 7% of each run, Pallas kernels for 0% -> 0%
where the time goes in v1:
time: 399 us
  waiting for transfers between devices  241 us (60%)
  matrix products  91.1 us (23%)
  other arithmetic  28.2 us (7%)
  blocking collectives  23.3 us (6%)
  between operations  15.6 us (4%)
    reduce_scatter x1, waiting for transfers between devices, local_head(): dh = lax.psum_scatter(dh, 'fsdp', scatter_dimension=0, tiled=True)  144 us
    all_gather x1, waiting for transfers between devices, local_head(): h_all = lax.all_gather(hidden, 'fsdp', axis=0, tiled=True)  56.2 us
    all_gather x1, waiting for transfers between devices, local_head(): stats = lax.all_gather(jnp.stack([row_max, row_sum, tgt]), 'fsdp', axis=0)  40 us
    dot_general x1, matrix products, local_head(): dh = jnp.dot(dz, weight, preferred_element_type=jnp.float32)  32.7 us
    dot_general x1, matrix products, local_head(): lax.dot_general(dz, h_all, (((0,), (0,)), ((), ())), preferred_element_ty...  29.8 us
    dot_general x1, matrix products, local_head(): lax.dot_general(h_all, weight, (((1,), (1,)), ((), ())), preferred_elemen...  28.7 us
    all_gather x1, blocking collectives, local_head(): t_all = lax.all_gather(targets, 'fsdp', axis=0, tiled=True)  23.3 us
    reduce_sum x1, other arithmetic, local_head(): row_sum = jnp.sum(jnp.exp(logits - row_max[:, None]), axis=1)  21.4 us
  transfers between devices with their start and end apart: 3, of which 3 were waited for; matrix products, arithmetic and copies ran while one was open for 7% of the time, Pallas kernels for 0%

profile of v1, /device:TPU:0, one launch (start us, length us, event | category | flops | bytes accessed | tf_op | source)
XLA Modules:
  0.0 399.0 jit_solution(13350529356122952524)
XLA Ops:
  7.2 0.0 copy-start
  7.2 0.0 all-gather.6.cloned.1.call-start
  7.2 0.7 all-gather.6.cloned.1.call-update
  7.9 0.0 all-gather.8.cloned.1.call-start
  8.0 23.3 %all-gather.1 = s32[16,1,512]{2,1,0:T(1,128)S(1)} all-gather(s32[1,1,512]{2,1,0:T(1,128)} %bitcast.33), channel_id=1, replica_groups=mesh['dp'=2,'fsdp'=16] {'fsdp'}, dimensions={0}, use_global_device_ids=true | all-gather | bytes 34816 | tf_op jit(solution)/shard_map/all_gather | solution.py:16
  31.3 56.2 %all-gather.6.cloned.1.call-done = bf16[8192,512]{1,0:T(8,128)(2,1)} async-done(((bf16[512,512]{1,0:T(8,128)(2,1)}), bf16[8192,512]{1,0:T(8,128)(2,1)}) %all-gather.6.cloned.1.call-update) | async-done | bytes 8388624 | tf_op jit(solution)/shard_map/all_gather | solution.py:15
  87.5 0.0 copy-done
  87.5 28.7 %fusion.7 = (f32[8192]{0:T(1024)S(1)}, f32[8192,2008]{0,1:T(8,128)}) fusion(bf16[8192,512]{1,0:T(8,128)(2,1)} %all-gather.6.cloned.1.call-done, bf16[2008,512]{1,0:T(8,128)(2,1)S(1)} %copy-done), kind=kOutput, calls=%fused_computation.18 | convolution fusion | flops 16860766208 | bytes 76275712 | tf_op jit(solution)/shard_map/dot_general | solution.py:17
  116.2 21.4 %exponential_reduce_fusion = (f32[8192]{0:T(1024)S(1)}, f32[8192]{0:T(1024)S(1)}) fusion(f32[8192,2008]{0,1:T(8,128)} %get-tuple-element.14, f32[8192]{0:T(1024)S(1)} %get-tuple-element.13, s32[8192]{0:T(1024)S(1)} %bitcast.29), kind=kLoop, calls=%fused_computation.3 | loop fusion | flops 82231296 | bytes 65929216 | tf_op jit(solution)/shard_map/reduce_sum | solution.py:20
  137.6 0.7 maximum_bitcast_fusion
  138.3 0.0 all-gather.8.cloned.1.call-update
  138.3 0.0 reduce-scatter.2.cloned.1.call-start
  138.4 40.0 %all-gather.8.cloned.1.call-done = f32[16,3,8192]{2,1,0:T(4,128)} async-done(((f32[1,3,8192]{2,1,0:T(4,128)}), f32[16,3,8192]{2,1,0:T(4,128)}) %all-gather.8.cloned.1.call-update) | async-done | bytes 1572880 | tf_op jit(solution)/shard_map/all_gather | solution.py:22
  178.4 4.7 %fusion.6 = (f32[16,1,8192]{2,1,0:T(1,128)S(1)}, f32[16,1,8192]{2,1,0:T(1,128)S(1)}, f32[8192]{0:T(1024)S(1)}, f32[8192]{0:T(1024)S(1)}) fusion(f32[16,3,8192]{2,1,0:T(4,128)} %all-gather.8.cloned.1.call-done), kind=kLoop, calls=%fused_computation.17 | loop fusion | flops 245760 | bytes 2686976 | tf_op jit(solution)/shard_map/slice | solution.py:24
  183.1 0.7 fusion.3
  183.8 0.6 subtract_reduce_fusion
  184.4 32.7 %fusion.5 = f32[8192,512]{1,0:T(8,128)} fusion(bf16[2008,512]{1,0:T(8,128)(2,1)S(1)} %copy-done, f32[8192,2008]{0,1:T(8,128)} %get-tuple-element.14, f32[8192]{0:T(1024)S(1)} %get-tuple-element.8, s32[8192]{0:T(1024)S(1)} %bitcast.30), kind=kOutput, calls=%fused_computation.16 | convolution fusion | flops 16943022080 | bytes 84697088 | tf_op jit(solution)/shard_map/dot_general | solution.py:27
  217.1 0.0 reduce-scatter.2.cloned.1.call-update
  217.8 29.8 %fusion.4 = f32[2008,512]{1,0:T(8,128)} fusion(bf16[8192,512]{1,0:T(8,128)(2,1)} %all-gather.6.cloned.1.call-done, f32[8192,2008]{0,1:T(8,128)} %get-tuple-element.14, f32[8192]{0:T(1024)S(1)} %get-tuple-element.8, s32[8192]{0:T(1024)S(1)} %bitcast.31), kind=kOutput, calls=%fused_computation.15 | convolution fusion | flops 16943022080 | bytes 78364672 | tf_op jit(solution)/shard_map/dot_general | solution.py:29
  247.5 143.9 %reduce-scatter.2.cloned.1.call-done = f32[512,512]{1,0:T(8,128)} async-done(((f32[8192,512]{1,0:T(8,128)}), f32[512,512]{1,0:T(8,128)}) %reduce-scatter.2.cloned.1.call-update) | async-done | bytes 1048592 | tf_op jit(solution)/shard_map/reduce_scatter | solution.py:28
  (1 shorter events, 0.0 us)
Async XLA Ops:
  7.2 80.3 %copy-start = (bf16[2008,512]{1,0:T(8,128)(2,1)S(1)}, bf16[2008,512]{1,0:T(8,128)(2,1)}, u32[]{:S(2)}) copy-start(bf16[2008,512]{1,0:T(8,128)(2,1)} %param.5) | copy-start | bytes 6168580
  7.2 80.3 %all-gather.6.cloned.1.call-start = ((), (), s32[]{:S(2)}) async-start(), calls=%async_computation.1 | async-start | bytes 8912896 | tf_op jit(solution)/shard_map/all_gather | solution.py:15
  7.9 170.5 %all-gather.8.cloned.1.call-start = ((), (), s32[]{:S(2)}) async-start(), calls=%async_computation.3 | async-start | bytes 2228224 | tf_op jit(solution)/shard_map/all_gather | solution.py:22
  138.3 253.0 %reduce-scatter.2.cloned.1.call-start = ((), (), s32[]{:S(2)}) async-start(), calls=%async_computation.2 | async-start | bytes 17825792 | tf_op jit(solution)/shard_map/reduce_scatter | solution.py:28
Sparse Core Ops, SparseCore 0:
  10.1 77.2 all-gather.5
  138.5 39.8 all-gather.7
  217.2 174.1 reduce-scatter.1

commit v2 on v1

v2 whole, which is shorter than its diff:
```python
import functools

import jax
import jax.numpy as jnp
from jax import lax
from jax.experimental import pallas as pl
from jax.experimental.pallas import tpu as pltpu
from jax.sharding import PartitionSpec as P

MESH = pl.DeviceIdType.MESH
BF16, F32 = jnp.bfloat16, jnp.float32
COLUMN = ((1, 2, 3), (2, 0, 3), (1, 3, 0), (2, 1, 0))
DESTS = ((3, 2, 1, 0), (3, 0, 2, 1), (0, 3, 1, 2), (0, 1, 2, 3))
PIECES = 4
SCHEDULE = (
    ("far", 0), ("near", 0), ("far", 1), ("hop", 0, 0), ("hop", 0, 1), ("near", 1), ("hop", 0, 2), ("hop", 0, 3),
    ("far", 2), ("hop", 1, 0), ("near", 2), ("hop", 1, 1), ("hop", 1, 2), ("far", 3), ("hop", 1, 3), ("hop", 2, 0),
    ("near", 3), ("dw_send",), ("hop", 2, 1), ("hop", 2, 2), ("hop", 2, 3), ("hop", 3, 0), ("dw_add",),
    ("hop", 3, 1), ("hop", 3, 2), ("hop", 3, 3),
)


def pick(z, table):
    lo, hi = z % 2, z // 2
    return table[0] * (1 - lo) * (1 - hi) + table[1] * lo * (1 - hi) + table[2] * (1 - lo) * hi + table[3] * lo * hi


def head_kernel(vocab, tile, h_ref, t_ref, w_ref, loss_ref, dht_ref, dw_out, x_all, xt_all, t_all, w_all, wt_all, dw, dw_in,
                far, near, far_in, chain, stats, lse, zt_row, loss_rows,
                x_recv, x_send, t_recv, t_send, w_sem, st_recv, st_send, ls_recv, ls_send, y_send, y_recv, c_send, c_recv,
                dw_sem, out_sem):
    tb, d = h_ref.shape
    vp = w_all.shape[0] // 2
    nt = vp // tile
    groups = tile // 8
    live = (vocab - (nt - 1) * tile) // 8
    qd = d // PIECES
    r = lax.axis_index("fsdp")
    c, chip = r % 2, r // 2
    y, z = chip % 2, chip // 2
    mate, across, left, right = r + 1 - 2 * c, r + 2 - 4 * y, r - 4, r + 4

    def remote(src, dst, ss, rs, dev):
        return pltpu.make_async_remote_copy(src_ref=src, dst_ref=dst, send_sem=ss, recv_sem=rs, device_id={"fsdp": dev}, device_id_type=MESH)

    def drain(ref, sem):
        pltpu.make_async_copy(ref, ref, sem).wait()

    barrier = pltpu.get_barrier_semaphore()
    for i in range(1, 16):
        pl.semaphore_signal(barrier, inc=1, device_id={"fsdp": (r + i) % 16}, device_id_type=MESH)

    w_all[pl.ds(vp - tile, tile), :] = jnp.zeros((tile, d), BF16)
    w_all[pl.ds(0, vocab), :] = w_ref[...]

    def transpose_w(i, _):
        wt_all[i] = w_all[pl.ds(pl.multiple_of(i * tile, tile), tile), :].T
        return 0

    lax.fori_loop(0, nt, transpose_w, 0)
    x_all[chip] = h_ref[...]
    t_all[chip] = t_ref[...]
    pl.semaphore_wait(barrier, 15)

    w_copy = remote(w_all.at[pl.ds(0, vp)], w_all.at[pl.ds(vp, vp)], w_sem.at[0], w_sem.at[1], mate)
    w_copy.start()

    def x_copy(dev, b, dirn, idx):
        return remote(x_all.at[b], x_all.at[b], x_send.at[dirn, idx], x_recv.at[b], dev)

    def t_copy(i):
        return remote(t_all.at[chip], t_all.at[chip], t_send, t_recv.at[chip], (2 * chip + 2 * i) % 16 + c)

    x_copy(across, chip, 0, 3).start()

    @pl.when(z > 0)
    def _():
        x_copy(left, chip, 1, 3).start()

    @pl.when(z < 3)
    def _():
        x_copy(right, chip, 2, 3).start()

    for i in range(1, 8):
        t_copy(i).start()
    w_copy.wait()
    lax.fori_loop(nt, 2 * nt, transpose_w, 0)

    def zero_dw(i, _):
        dw[pl.ds(pl.multiple_of(i * tile, tile), tile), :] = jnp.zeros((tile, d), F32)
        return 0

    lax.fori_loop(0, 2 * nt, zero_dw, 0)

    iota8 = lax.broadcasted_iota(jnp.int32, (8, tb), 0)
    group8 = lax.broadcasted_iota(jnp.int32, (groups, 8, tb), 0) * 8

    def target_rows(b, i):
        slot = i // nt
        rel = t_all[b] - vocab * (r * (1 - slot) + mate * slot)
        rel = jnp.where((rel >= 0) & (rel < vocab), rel, -vp)
        return jnp.broadcast_to(rel - (i % nt) * tile, (8, tb)) - iota8

    def tile_logits(b, i):
        rows = pl.ds(pl.multiple_of(i * tile, tile), tile)
        return jnp.dot(w_all[rows, :], xt_all[b], preferred_element_type=F32).reshape(groups, 8, tb)

    def mask_pad(vals, i, fill):
        if live == groups:
            return vals
        tail = jnp.where((jnp.zeros((groups - live, 8, tb), jnp.int32) + i % nt) == nt - 1, fill, vals[live:])
        return jnp.concatenate([vals[:live], tail], axis=0)

    zt_row[...] = jnp.zeros_like(zt_row)

    def forward(step, codes):
        code_z, code_y = codes
        zs, flip = code_z % 4, code_y % 2
        b = 2 * zs + y + flip * (1 - 2 * y)

        @pl.when(step > 0)
        def _():
            drain(x_all.at[b], x_recv.at[b])
            drain(t_all.at[b], t_recv.at[b])

        @pl.when((step > 0) & (flip == 0))
        def _():
            k = (step - 1) // 2
            x_copy(across, b, 0, k).start()

            @pl.when((zs > z) & (z > 0))
            def _():
                x_copy(left, b, 1, k).start()

            @pl.when((zs < z) & (z < 3))
            def _():
                x_copy(right, b, 2, k).start()

        xt_all[b] = x_all[b].T

        def tile_step(i, carry):
            m, s, zt = carry
            zv = tile_logits(b, i)
            hit = target_rows(b, i)[None] == group8
            zt = zt + jnp.sum(jnp.where(hit, zv, 0.0), axis=0)
            zv = mask_pad(zv, i, -jnp.inf)
            m_new = jnp.maximum(m, jnp.max(zv, axis=0))
            s = s * jnp.exp(m - m_new) + jnp.sum(jnp.exp(zv - m_new[None]), axis=0)
            return m_new, s, zt

        zero = jnp.zeros((8, tb), F32)
        m, s, zt = lax.fori_loop(0, 2 * nt, tile_step, (jnp.full((8, tb), -jnp.inf, F32), zero, zero))
        m1 = jnp.max(m, axis=0, keepdims=True)
        s1 = jnp.sum(s * jnp.exp(m - m1), axis=0, keepdims=True)
        stats[chip, b] = jnp.concatenate([m1, s1], axis=0)
        zt_row[...] += jnp.sum(zt, axis=0, keepdims=True)
        for i in range(1, 8):
            remote(stats.at[chip, b], stats.at[chip, b], st_send, st_recv.at[chip], (2 * chip + 2 * i) % 16 + c).start()
        return code_z // 4, code_y // 2

    zlists = [(q, COLUMN[q][0], q, COLUMN[q][1], COLUMN[q][0], COLUMN[q][2], COLUMN[q][1], COLUMN[q][2]) for q in range(4)]
    code_z = pick(z, [sum(v * 4**s for s, v in enumerate(zl)) for zl in zlists])
    code_y = sum(v * 2**s for s, v in enumerate((0, 0, 1, 0, 1, 0, 1, 1)))
    lax.fori_loop(0, 8, forward, (code_z, jnp.int32(code_y)))

    for i in range(1, 8):
        src = (chip + i) % 8
        drain(stats.at[src], st_recv.at[src])

    def combine(b, _):
        ms = [stats[q, b][0:1] for q in range(8)]
        top = functools.reduce(jnp.maximum, ms)
        tot = sum(stats[q, b][1:2] * jnp.exp(ms[q] - top) for q in range(8))
        lse[b] = top + jnp.log(tot)
        return 0

    lax.fori_loop(0, 8, combine, 0)
    loss_rows[r] = lse[chip] - zt_row[...]

    def loss_copy(i):
        return remote(loss_rows.at[r], loss_rows.at[r], ls_send, ls_recv, (r + i) % 16)

    for i in range(1, 16):
        loss_copy(i).start()

    def backward(b, acc):
        acc[...] = jnp.zeros((d, tb), F32)
        norm = jnp.broadcast_to(lse[b], (8, tb))[None]

        def tile_step(i, _):
            rows = pl.ds(pl.multiple_of(i * tile, tile), tile)
            prob = jnp.exp(tile_logits(b, i) - norm)
            hit = target_rows(b, i)[None] == group8
            dz = mask_pad(prob - jnp.where(hit, 1.0, 0.0), i, 0.0)
            dz = dz.reshape(tile, tb).astype(BF16)
            acc[...] += jnp.dot(wt_all[i], dz, preferred_element_type=F32)
            dw[rows, :] += jnp.dot(dz, x_all[b], preferred_element_type=F32)
            return 0

        lax.fori_loop(0, 2 * nt, tile_step, 0)

    def dest(k):
        return pick(z, [DESTS[q][k] for q in range(4)])

    def y_copy(k, q):
        rows = pl.ds(q * qd, qd)
        return remote(far.at[k, rows], far_in.at[k, rows], y_send.at[k, q], y_recv.at[k, q], across)

    def chain_copy(k, q, slot, dev):
        rows = pl.ds(q * qd, qd)
        return remote(near.at[k, rows], chain.at[slot, rows], c_send.at[k, q], c_recv.at[slot, q], dev)

    def hop(k, q):
        zd = dest(k)
        rows = pl.ds(q * qd, qd)
        y_copy(k, q).wait_recv()
        near[k, rows] = near[k, rows] + far_in[k, rows]

        def add_chain(slot):
            drain(chain.at[slot, rows], c_recv.at[slot, q])
            near[k, rows] = near[k, rows] + chain[slot, rows]

        if k < 3:
            @pl.when(((zd > z) & (z > 0)) | ((zd < z) & (z < 3)))
            def _():
                add_chain(zd)

            @pl.when(zd > z)
            def _():
                chain_copy(k, q, zd, right).start()

            @pl.when(zd == z - 1)
            def _():
                chain_copy(k, q, 4, left).start()

            @pl.when(zd < z - 1)
            def _():
                chain_copy(k, q, zd, left).start()
        else:
            @pl.when(z > 0)
            def _():
                add_chain(z)

            @pl.when(z < 3)
            def _():
                add_chain(4)

            pltpu.make_async_copy(near.at[k, rows], dht_ref.at[rows], out_sem.at[q]).start()

    dw_copy = remote(dw.at[pl.ds(vp, vp)], dw_in, dw_sem.at[0], dw_sem.at[1], mate)
    dw_store = pltpu.make_async_copy(dw.at[pl.ds(0, vocab)], dw_out, out_sem.at[PIECES])
    for event in SCHEDULE:
        if event[0] == "far":
            backward(2 * dest(event[1]) + 1 - y, far.at[event[1]])
            for q in range(PIECES):
                y_copy(event[1], q).start()
        elif event[0] == "near":
            backward(2 * dest(event[1]) + y, near.at[event[1]])
        elif event[0] == "hop":
            hop(*event[1:])
        elif event[0] == "dw_send":
            dw_copy.start()
        else:
            dw_copy.wait_recv()

            def add_dw(i, _):
                rows = pl.ds(pl.multiple_of(i * tile, tile), tile)
                dw[rows, :] += dw_in[rows, :]
                return 0

            lax.fori_loop(0, nt, add_dw, 0)
            dw_store.start()

    drain(loss_rows.at[pl.ds(0, 15)], ls_recv)
    total = sum(loss_rows[q] for q in range(16))
    loss_ref[...] = jnp.sum(total, axis=1, keepdims=True) * jnp.ones((1, 128), F32)

    drain(loss_rows.at[pl.ds(0, 15)], ls_send)
    drain(stats.at[pl.ds(0, 7)], st_send)
    drain(t_all.at[pl.ds(0, 7)], t_send)
    x_copy(across, chip, 0, 3).wait_send()

    @pl.when(z > 0)
    def _():
        x_copy(left, chip, 1, 3).wait_send()

    @pl.when(z < 3)
    def _():
        x_copy(right, chip, 2, 3).wait_send()

    for k in range(3):
        zs = pick(z, [COLUMN[q][k] for q in range(4)])
        x_copy(across, chip, 0, k).wait_send()

        @pl.when((zs > z) & (z > 0))
        def _():
            x_copy(left, chip, 1, k).wait_send()

        @pl.when((zs < z) & (z < 3))
        def _():
            x_copy(right, chip, 2, k).wait_send()

        for q in range(PIECES):
            drain(near.at[k, pl.ds(q * qd, qd)], c_send.at[k, q])
    for k in range(4):
        for q in range(PIECES):
            y_copy(k, q).wait_send()
    dw_copy.wait_send()
    dw_store.wait()
    for q in range(PIECES):
        rows = pl.ds(q * qd, qd)
        pltpu.make_async_copy(near.at[3, rows], dht_ref.at[rows], out_sem.at[q]).wait()


def solution(mesh, tile=512):
    groups = mesh.shape["fsdp"]
    tok_spec = P(("dp", "fsdp"), None)

    def local_head(hidden, targets, weight):
        tb, d = hidden.shape
        vocab = weight.shape[0]
        vp = -(-vocab // tile) * tile
        nt = vp // tile
        dma = pltpu.SemaphoreType.DMA
        vmem = pltpu.VMEM
        loss, dht, dw = pl.pallas_call(
            functools.partial(head_kernel, vocab, tile),
            out_shape=(jax.ShapeDtypeStruct((1, 128), F32), jax.ShapeDtypeStruct((d, tb), F32), jax.ShapeDtypeStruct((vocab, d), F32)),
            in_specs=[pl.BlockSpec(memory_space=vmem)] * 3,
            out_specs=(pl.BlockSpec(memory_space=vmem), pl.BlockSpec(memory_space=pl.ANY), pl.BlockSpec(memory_space=pl.ANY)),
            scratch_shapes=[
                vmem((8, tb, d), BF16), vmem((8, d, tb), BF16), vmem((8, 1, tb), jnp.int32),
                vmem((2 * vp, d), BF16), vmem((2 * nt, d, tile), BF16),
                vmem((2 * vp, d), F32), vmem((vp, d), F32),
                vmem((4, d, tb), F32), vmem((4, d, tb), F32), vmem((4, d, tb), F32), vmem((5, d, tb), F32),
                vmem((8, 8, 2, tb), F32), vmem((8, 1, tb), F32), vmem((1, tb), F32), vmem((16, 1, tb), F32),
                dma((8,)), dma((3, 4)), dma((8,)), dma, dma((2,)), dma((8,)), dma, dma, dma,
                dma((4, PIECES)), dma((4, PIECES)), dma((3, PIECES)), dma((5, PIECES)), dma((2,)), dma((PIECES + 1,)),
            ],
            compiler_params=pltpu.CompilerParams(collective_id=0, has_side_effects=True, vmem_limit_bytes=66_000_000),
        )(hidden, targets.reshape(1, tb), weight)
        scale = 1.0 / (tb * groups)
        return loss[0, :1] * scale, dht.T * scale, dw * scale

    return jax.shard_map(local_head, mesh=mesh, in_specs=(tok_spec, P(("dp", "fsdp")), P("fsdp", None)), out_specs=(P("dp"), tok_spec, tok_spec), check_vma=False)
```

time: 399 us -> 189 us (0.47)
  waiting for transfers between devices: 241 us -> 0 us
  Pallas kernels: 0 us -> 177 us
  matrix products: 91.1 us -> 0 us
  blocking collectives: 23.3 us -> 0 us
  other arithmetic: 28.2 us -> 5.95 us
  between operations: 15.6 us -> 2.41 us
    pallas_call x0 -> x1, Pallas kernels: none -> 177 us  [local_head(): pl.pallas_call(functools.partial(head_kernel, vocab, tile), out_shape=(ja...]
    reduce_scatter x1 -> x0, waiting for transfers between devices: 144 us -> none  [local_head(): dh = lax.psum_scatter(dh, 'fsdp', scatter_dimension=0, tiled=True)]
    all_gather x2 -> x0, waiting for transfers between devices: 96.2 us -> none  [the longest x1 56.2 us: local_head(): h_all = lax.all_gather(hidden, 'fsdp', axis=0, tiled=True)]
    dot_general x3 -> x0, matrix products: 91.1 us -> none  [the longest x1 32.7 us: local_head(): dh = jnp.dot(dz, weight, preferred_element_type=jnp.float32)]
    all_gather x1 -> x0, blocking collectives: 23.3 us -> none  [local_head(): t_all = lax.all_gather(targets, 'fsdp', axis=0, tiled=True)]
    reduce_sum x3 -> x0, other arithmetic: 22.7 us -> none  [the longest x1 21.4 us: local_head(): row_sum = jnp.sum(jnp.exp(logits - row_max[:, None]), axis=1)]
    mul x0 -> x2, other arithmetic: none -> 5.95 us  [local_head(): return (loss[0, :1] * scale, dht.T * scale, dw * scale)]
    slice x1 -> x0, other arithmetic: 4.73 us -> none  [local_head(): stats[:, 1] * jnp.exp(stats[:, 0] - all_max)]
  transfers between devices with their start and end apart: 3 -> 0, of which waited for: 3 -> 0; matrix products, arithmetic and copies ran while one was open for 7% -> 0% of each run, Pallas kernels for 0% -> 0%
where the time goes in v2:
time: 189 us; the launch traced here: 186 us
  Pallas kernels  177 us (94%)
  other arithmetic  5.95 us (3%)
  between operations  2.41 us (1%)
    pallas_call x1, Pallas kernels, local_head(): pl.pallas_call(functools.partial(head_kernel, vocab, tile), out_shape=(ja...  177 us
    mul x2, other arithmetic, local_head(): return (loss[0, :1] * scale, dht.T * scale, dw * scale)  5.95 us

profile of v2, /device:TPU:0, one launch (start us, length us, event | category | flops | bytes accessed | tf_op | source)
XLA Modules:
  0.0 186.3 jit_solution(645875023797571699)
XLA Ops:
  0.6 176.6 %shard_map.58 = (f32[1,128]{1,0:T(1,128)}, f32[512,512]{1,0:T(8,128)}, f32[2008,512]{1,0:T(8,128)}) custom-call(bf16[512,512]{1,0:T(8,128)(2,1)} %h_ref.1, s32[1,512]{1,0:T(1,128)} %bitcast.5, bf16[2008,512]{1,0:T(8,128)(2,1)} %w_ref.1), custom_call_target="tpu_custom_call" | custom-call | tf_op jit(solution)/shard_map/pallas_call | solution.py:326
  177.9 1.3 multiply_bitcast_fusion
  179.2 1.3 copy.6
  180.5 4.6 %broadcast_multiply_fusion = f32[2008,512]{1,0:T(8,128)} fusion(f32[2008,512]{1,0:T(8,128)} %get-tuple-element.8), kind=kLoop, calls=%fused_computation | loop fusion | flops 1028096 | bytes 8224768 | tf_op jit(solution)/shard_map/mul | solution.py:343

commit v3 on v1

v3 whole, which is shorter than its diff:
```python
import functools

import jax
import jax.numpy as jnp
from jax import lax
from jax.experimental import pallas as pl
from jax.experimental.pallas import tpu as pltpu
from jax.sharding import PartitionSpec as P

MESH = pl.DeviceIdType.MESH
BF16, F32 = jnp.bfloat16, jnp.float32
CHUNKS = 4
COLUMN = ((1, 2, 3), (2, 0, 3), (1, 3, 0), (2, 1, 0))
DESTS = ((3, 2, 1, 0), (3, 2, 0, 1), (0, 1, 3, 2), (0, 1, 2, 3))
Y_FIRST = (0, 0, 1, 1)
SCHEDULE = (
    ('A', 'own', 0), ('E', 'own', 2), ('I', 'ag', 0, 2), ('A', 'ag', 0, 0), ('E', 'own', 1), ('E', 'ag', 0, 2),
    ('I', 'own', 1), ('E', 'ag', 2, 0), ('A', 'prep', 2.5), ('I', 'ag', 0, 1), ('A', 'ag', 0, 4), ('I', 'ag', 1, 2),
    ('E', 'ag', 1, 0), ('A', 'fwd', 0, 0), ('E', 'own', 3), ('I', 'ag', 1, 0), ('I', 'own', 2), ('I', 'ag', 0, 6),
    ('I', 'ag', 1, 4), ('E', 'ag', 0, 1), ('E', 'ag', 0, 6), ('I', 'ag', 0, 5), ('E', 'ag', 0, 3), ('E', 'ag', 0, 5),
    ('I', 'ag', 0, 3), ('I', 'ag', 2, 3), ('I', 'ag', 1, 1), ('I', 'ag', 2, 1), ('A', 'fwd', 0, 1), ('E', 'ag', 1, 3),
    ('E', 'ag', 1, 4), ('I', 'ag', 2, 4), ('E', 'ag', 1, 2), ('I', 'ag', 2, 0), ('I', 'ag', 2, 6), ('A', 'stat', 0),
    ('I', 'own', 3), ('A', 'bwd', 0, 1, 0), ('E', 'ag', 2, 1), ('E', 'ag', 3, 0), ('A', 'bwd', 0, 1, 1),
    ('I', 'ag', 1, 6), ('E', 'ag', 1, 1), ('I', 'ag', 1, 3), ('I', 'ag', 1, 5), ('A', 'bwd', 0, 0, 0),
    ('I', 'ag', 2, 2), ('I', 'ag', 3, 4), ('E', 'ag', 1, 5), ('E', 'ag', 1, 6), ('A', 'fwd', 1, 1), ('I', 'ag', 3, 0),
    ('E', 'ag', 2, 2), ('A', 'fwd', 1, 0), ('I', 'ag', 3, 3), ('A', 'bwd', 0, 0, 1), ('E', 'hop', 0, 1),
    ('A', 'stat', 1), ('I', 'ag', 2, 5), ('I', 'ag', 3, 6), ('A', 'bwd', 1, 1, 0), ('E', 'ag', 2, 6),
    ('E', 'hop', 0, 0), ('A', 'bwd', 1, 1, 1), ('E', 'ag', 2, 3), ('E', 'ag', 2, 5), ('I', 'ag', 3, 1),
    ('A', 'fwd', 2, 0), ('A', 'bwd', 1, 0, 0), ('I', 'ag', 3, 2), ('E', 'ag', 3, 1), ('E', 'ag', 2, 4),
    ('I', 'ag', 3, 5), ('I', 'hop', 0, 1), ('I', 'hop', 0, 0), ('A', 'fwd', 2, 1), ('A', 'bwd', 1, 0, 1),
    ('E', 'ag', 3, 4), ('E', 'ag', 3, 6), ('A', 'stat', 2), ('E', 'hop', 1, 0), ('E', 'ag', 3, 3),
    ('A', 'bwd', 2, 1, 0), ('E', 'hop', 1, 1), ('A', 'bwd', 2, 1, 1), ('E', 'ag', 3, 5), ('A', 'bwd', 2, 0, 0),
    ('E', 'ag', 3, 2), ('E', 'hop', 1, 2), ('A', 'fwd', 3, 1), ('I', 'hop', 0, 2), ('A', 'fwd', 3, 0),
    ('I', 'hop', 1, 0), ('E', 'hop', 0, 2), ('A', 'bwd', 2, 0, 1), ('E', 'hop', 2, 0), ('I', 'hop', 1, 1),
    ('A', 'stat', 3), ('A', 'bwd', 3, 1, 0), ('A', 'bwd', 3, 0, 0), ('E', 'hop', 2, 1), ('A', 'bwd', 3, 1, 1),
    ('E', 'hop', 2, 2), ('I', 'hop', 2, 0), ('A', 'bwd', 3, 0, 1), ('A', 'dw_send'), ('I', 'hop', 1, 2),
    ('I', 'hop', 2, 1), ('A', 'hop', 3, 0), ('I', 'hop', 0, 3), ('I', 'hop', 2, 2), ('I', 'hop', 3, 1),
    ('I', 'hop', 2, 3), ('I', 'hop', 3, 2), ('E', 'hop', 1, 3), ('E', 'hop', 0, 3), ('E', 'hop', 3, 1),
    ('E', 'hop', 3, 2), ('E', 'hop', 2, 3), ('E', 'hop', 3, 3), ('A', 'dw_add'), ('I', 'hop', 1, 3),
    ('I', 'hop', 3, 3),
)


def pick(z, table):
    lo, hi = z % 2, z // 2
    return table[0] * (1 - lo) * (1 - hi) + table[1] * lo * (1 - hi) + table[2] * (1 - lo) * hi + table[3] * lo * hi


def head_kernel(vocab, tile, h_ref, t_ref, w_ref, loss_ref, dht_ref, dw_out, x_all, xt_all, t_all, w_all, wt_all, dw, dw_in,
                far, near, far_in, chain, stats, lse, zt_acc, loss_rows,
                x_recv, x_send, t_recv, t_send, w_sem, st_recv, st_send, ls_recv, ls_send, y_send, y_recv, c_send, c_recv,
                dw_sem, out_sem):
    tb, d = h_ref.shape
    tc = tb // CHUNKS
    vp = w_all.shape[0] // 2
    nt = vp // tile
    groups = tile // 8
    live = (vocab - (nt - 1) * tile) // 8
    r = lax.axis_index("fsdp")
    c, chip = r % 2, r // 2
    y, z = chip % 2, chip // 2
    mate, across, left, right = r + 1 - 2 * c, r + 2 - 4 * y, r - 4, r + 4

    def remote(src, dst, ss, rs, dev):
        return pltpu.make_async_remote_copy(src_ref=src, dst_ref=dst, send_sem=ss, recv_sem=rs, device_id={"fsdp": dev}, device_id_type=MESH)

    def drain(ref, sem):
        pltpu.make_async_copy(ref, ref, sem).wait()

    barrier = pltpu.get_barrier_semaphore()
    for i in range(1, 16):
        pl.semaphore_signal(barrier, inc=1, device_id={"fsdp": (r + i) % 16}, device_id_type=MESH)

    for k in range(CHUNKS):
        x_all[2 * k, z] = h_ref[k * tc:(k + 1) * tc, :]
    t_all[chip] = t_ref[...]
    w_all[pl.ds(vp - tile, tile), :] = jnp.zeros((tile, d), BF16)
    w_all[pl.ds(0, vocab), :] = w_ref[...]

    def transpose_w(i, _):
        wt_all[i] = w_all[pl.ds(pl.multiple_of(i * tile, tile), tile), :].T
        return 0

    def zero_dw(i, _):
        dw[pl.ds(pl.multiple_of(i * tile, tile), tile), :] = jnp.zeros((tile, d), F32)
        return 0

    lax.fori_loop(0, nt, transpose_w, 0)
    pl.semaphore_wait(barrier, 15)

    w_copy = remote(w_all.at[pl.ds(0, vp)], w_all.at[pl.ds(vp, vp)], w_sem.at[0], w_sem.at[1], mate)

    def t_copy(i):
        return remote(t_all.at[chip], t_all.at[chip], t_send, t_recv, (2 * chip + 2 * i) % 16 + c)

    def prepare():
        for i in range(1, 8):
            t_copy(i).start()
        w_copy.start()
        lax.fori_loop(0, 2 * nt, zero_dw, 0)
        zt_acc[...] = jnp.zeros_like(zt_acc)
        w_copy.wait()
        lax.fori_loop(nt, 2 * nt, transpose_w, 0)

    def x_copy(k, col, zs, way, slot):
        dev = (across, left, right)[way]
        to = 1 if way == 0 else col
        return remote(x_all.at[2 * k + col, zs], x_all.at[2 * k + to, zs], x_send.at[way, k, slot], x_recv.at[2 * k + to, zs], dev)

    def along(k, col, zs, slot, to_left, to_right, act):
        @pl.when(to_left)
        def _():
            act(x_copy(k, col, zs, 1, slot))

        @pl.when(to_right)
        def _():
            act(x_copy(k, col, zs, 2, slot))

    def own(k, act):
        act(x_copy(k, 0, z, 0, 7))
        along(k, 0, z, 7, z > 0, z < 3, act)

    def arrival(k, j):
        if Y_FIRST[k]:
            col, n = (1, 0, 1, 0, 1, 0, 1)[j], (None, 0, 0, 1, 1, 2, 2)[j]
        else:
            col, n = (0, 1, 0, 1, 0, 1, 1)[j], (0, None, 1, 0, 2, 1, 2)[j]
        return col, z if n is None else pick(z, [COLUMN[q][n] for q in range(4)])

    def relay(k, j, act):
        col, zs = arrival(k, j)
        if Y_FIRST[k]:
            along(k, col, zs, j, (zs >= z) & (z > 0), (zs <= z) & (z < 3), act)
        elif col == 0:
            act(x_copy(k, 0, zs, 0, j))
            along(k, 0, zs, j, (zs > z) & (z > 0), (zs < z) & (z < 3), act)

    def gather(k, j):
        col, zs = arrival(k, j)
        drain(x_all.at[2 * k + col, zs], x_recv.at[2 * k + col, zs])
        relay(k, j, lambda copy: copy.start())

    def tile_logits(b, i):
        rows = pl.ds(pl.multiple_of(i * tile, tile), tile)
        return jnp.dot(w_all[rows, :], xt_all[b], preferred_element_type=F32).reshape(groups, 8, tb)

    def mask_pad(vals, i, fill):
        if live == groups:
            return vals
        tail = jnp.where((jnp.zeros((groups - live, 8, tb), jnp.int32) + i % nt) == nt - 1, fill, vals[live:])
        return jnp.concatenate([vals[:live], tail], axis=0)

    def place(k, col):
        return 2 * k + y + col * (1 - 2 * y)

    def forward(k, col):
        b = 2 * k + col
        xt_all[b] = x_all[b].reshape(tb, d).T

        def tile_step(i, carry):
            m, s = carry
            zv = mask_pad(tile_logits(b, i), i, -jnp.inf)
            m_new = jnp.maximum(m, jnp.max(zv, axis=0))
            s = s * jnp.exp(m - m_new) + jnp.sum(jnp.exp(zv - m_new[None]), axis=0)
            return m_new, s

        m, s = lax.fori_loop(0, 2 * nt, tile_step, (jnp.full((8, tb), -jnp.inf, F32), jnp.zeros((8, tb), F32)))
        m1 = jnp.max(m, axis=0, keepdims=True)
        s1 = jnp.sum(s * jnp.exp(m - m1), axis=0, keepdims=True)
        p = place(k, col)
        stats[chip, p] = jnp.concatenate([m1, s1], axis=0)
        for i in range(1, 8):
            remote(stats.at[chip, p], stats.at[chip, p], st_send, st_recv.at[k], (2 * chip + 2 * i) % 16 + c).start()

    def combine(k):
        drain(stats.at[pl.ds(0, 7), pl.ds(0, 2)], st_recv.at[k])
        for b in (2 * k, 2 * k + 1):
            both = [stats[q, b] for q in range(8)]
            top = functools.reduce(jnp.maximum, [v[0:1] for v in both])
            tot = sum(v[1:2] * jnp.exp(v[0:1] - top) for v in both)
            lse[b] = top + jnp.log(tot)

    iota8 = lax.broadcasted_iota(jnp.int32, (8, tb), 0)
    group8 = lax.broadcasted_iota(jnp.int32, (groups, 8, tb), 0) * 8

    def backward(k, col, half):
        b = 2 * k + col
        acc = far if col else near
        phys = y + col * (1 - 2 * y)
        if half == 0:
            acc[k] = jnp.zeros((4, d, tc), F32)
        norm = jnp.broadcast_to(lse[place(k, col)], (8, tb))[None]
        ids = jnp.concatenate([t_all[2 * q + phys][:, k * tc:(k + 1) * tc] for q in range(4)], axis=1)
        rel = ids - vocab * (mate if half else r)
        rel = jnp.where((rel >= 0) & (rel < vocab), rel, -2 * vp)
        rel8 = jnp.broadcast_to(rel, (8, tb)) - iota8

        def tile_step(i, _):
            rows = pl.ds(pl.multiple_of(i * tile, tile), tile)
            zv = tile_logits(b, i)
            hit = (rel8 - (i - half * nt) * tile)[None] == group8
            zt_acc[...] += jnp.sum(jnp.where(hit, zv, 0.0), axis=0)
            dz = mask_pad(jnp.exp(zv - norm) - jnp.where(hit, 1.0, 0.0), i, 0.0)
            dz = dz.reshape(tile, tb).astype(BF16)
            part = jnp.dot(wt_all[i], dz, preferred_element_type=F32)
            for q in range(4):
                acc[k, q] += part[:, q * tc:(q + 1) * tc]
            dw[rows, :] += jnp.dot(dz, x_all[b].reshape(tb, d), preferred_element_type=F32)
            return 0

        lax.fori_loop(half * nt, (half + 1) * nt, tile_step, 0)
        if col == 1 and half == 1:
            for j in range(4):
                y_copy(k, dest(j)).start()

    def dest(j):
        return pick(z, [DESTS[q][j] for q in range(4)])

    def y_copy(k, zd):
        return remote(far.at[k, zd], far_in.at[k, zd], y_send.at[k, zd], y_recv.at[k, zd], across)

    def hop(k, j):
        zd = dest(j)
        drain(far_in.at[k, zd], y_recv.at[k, zd])

        def add_chain(slot):
            drain(chain.at[k, slot], c_recv.at[k, slot])
            near[k, zd] = near[k, zd] + far_in[k, zd] + chain[k, slot]

        def send(slot, dev):
            remote(near.at[k, zd], chain.at[k, slot], c_send.at[k, j], c_recv.at[k, slot], dev).start()

        if j < 3:
            passing = ((zd > z) & (z > 0)) | ((zd < z) & (z < 3))

            @pl.when(passing)
            def _():
                add_chain(zd)

            @pl.when(jnp.logical_not(passing))
            def _():
                near[k, zd] = near[k, zd] + far_in[k, zd]

            @pl.when(zd > z)
            def _():
                send(zd, right)

            @pl.when(zd == z - 1)
            def _():
                send(4, left)

            @pl.when(zd < z - 1)
            def _():
                send(zd, left)
        else:
            @pl.when((z > 0) & (z < 3))
            def _():
                drain(chain.at[k, z], c_recv.at[k, z])
                drain(chain.at[k, 4], c_recv.at[k, 4])
                near[k, z] = (near[k, z] + far_in[k, z]) + (chain[k, z] + chain[k, 4])

            @pl.when(z == 0)
            def _():
                add_chain(4)

            @pl.when(z == 3)
            def _():
                add_chain(3)

            out_copy(k).start()

    def out_copy(k):
        return pltpu.make_async_copy(near.at[k, z], dht_ref.at[k], out_sem.at[k])

    dw_copy = remote(dw.at[pl.ds(vp, vp)], dw_in, dw_sem.at[0], dw_sem.at[1], mate)
    dw_store = pltpu.make_async_copy(dw.at[pl.ds(0, vocab)], dw_out, out_sem.at[CHUNKS])

    def loss_copy(i):
        return remote(loss_rows.at[r], loss_rows.at[r], ls_send, ls_recv, (r + i) % 16)

    def send_grads():
        dw_copy.start()
        rows = sum(lse[b] for b in range(8)) * jnp.where(chip == 0, 1.0, 0.0)
        loss_rows[r] = rows - jnp.sum(zt_acc[...], axis=0, keepdims=True)
        for i in range(1, 16):
            loss_copy(i).start()

    def add_dw():
        dw_copy.wait_recv()

        def step(i, _):
            rows = pl.ds(pl.multiple_of(i * tile, tile), tile)
            dw[rows, :] += dw_in[rows, :]
            return 0

        lax.fori_loop(0, nt, step, 0)
        dw_store.start()
        drain(loss_rows.at[pl.ds(0, 15)], ls_recv)
        total = sum(loss_rows[q] for q in range(16))
        loss_ref[...] = jnp.sum(total, axis=1, keepdims=True) * jnp.ones((1, 128), F32)

    def start(copy):
        copy.start()

    first_backward = [e[1] for e in SCHEDULE].index("bwd")
    for n, (who, kind, *args) in enumerate(SCHEDULE):
        if n == first_backward:
            drain(t_all.at[pl.ds(0, 7)], t_recv)

        def run(kind=kind, args=args):
            if kind == "own":
                own(args[0], start)
            elif kind == "ag":
                gather(*args)
            elif kind == "hop":
                hop(*args)
            elif kind == "prep":
                prepare()
            elif kind == "fwd":
                forward(*args)
            elif kind == "stat":
                combine(*args)
            elif kind == "bwd":
                backward(*args)
            elif kind == "dw_send":
                send_grads()
            else:
                add_dw()

        if who == "A":
            run()
        else:
            pl.when(((z == 0) | (z == 3)) if who == "E" else ((z == 1) | (z == 2)))(run)

    def finish(copy):
        copy.wait_send()

    drain(loss_rows.at[pl.ds(0, 15)], ls_send)
    drain(stats.at[pl.ds(0, 7)], st_send)
    drain(t_all.at[pl.ds(0, 7)], t_send)
    for k in range(CHUNKS):
        own(k, finish)
        for j in range(7):
            relay(k, j, finish)
        for zd in range(4):
            y_copy(k, zd).wait_send()
        for j in range(3):
            drain(near.at[k, 0], c_send.at[k, j])
        out_copy(k).wait()
    dw_copy.wait_send()
    dw_store.wait()


def solution(mesh, tile=512):
    groups = mesh.shape["fsdp"]
    tok_spec = P(("dp", "fsdp"), None)

    def local_head(hidden, targets, weight):
        tb, d = hidden.shape
        tc = tb // CHUNKS
        vocab = weight.shape[0]
        vp = -(-vocab // tile) * tile
        nt = vp // tile
        dma = pltpu.SemaphoreType.DMA
        vmem = pltpu.VMEM
        loss, dht, dw = pl.pallas_call(
            functools.partial(head_kernel, vocab, tile),
            out_shape=(jax.ShapeDtypeStruct((1, 128), F32), jax.ShapeDtypeStruct((CHUNKS, d, tc), F32), jax.ShapeDtypeStruct((vocab, d), F32)),
            in_specs=[pl.BlockSpec(memory_space=vmem)] * 3,
            out_specs=(pl.BlockSpec(memory_space=vmem), pl.BlockSpec(memory_space=pl.ANY), pl.BlockSpec(memory_space=pl.ANY)),
            scratch_shapes=[
                vmem((8, 4, tc, d), BF16), vmem((8, d, tb), BF16), vmem((8, 1, tb), jnp.int32),
                vmem((2 * vp, d), BF16), vmem((2 * nt, d, tile), BF16),
                vmem((2 * vp, d), F32), vmem((vp, d), F32),
                vmem((CHUNKS, 4, d, tc), F32), vmem((CHUNKS, 4, d, tc), F32), vmem((CHUNKS, 4, d, tc), F32), vmem((CHUNKS, 5, d, tc), F32),
                vmem((8, 8, 2, tb), F32), vmem((8, 1, tb), F32), vmem((8, tb), F32), vmem((16, 1, tb), F32),
                dma((8, 4)), dma((3, CHUNKS, 8)), dma, dma, dma((2,)), dma((CHUNKS,)), dma, dma, dma,
                dma((CHUNKS, 4)), dma((CHUNKS, 4)), dma((CHUNKS, 3)), dma((CHUNKS, 5)), dma((2,)), dma((CHUNKS + 1,)),
            ],
            compiler_params=pltpu.CompilerParams(collective_id=0, has_side_effects=True, vmem_limit_bytes=66_000_000),
        )(hidden, targets.reshape(1, tb), weight)
        scale = 1.0 / (tb * groups)
        dh = dht.transpose(0, 2, 1).reshape(tb, d)
        return loss[0, :1] * scale, dh * scale, dw * scale

    return jax.shard_map(local_head, mesh=mesh, in_specs=(tok_spec, P(("dp", "fsdp")), P("fsdp", None)), out_specs=(P("dp"), tok_spec, tok_spec), check_vma=False)
```

time: 399 us -> 192 us (0.48)
  waiting for transfers between devices: 241 us -> 0 us
  Pallas kernels: 0 us -> 182 us
  matrix products: 91.1 us -> 0 us
  blocking collectives: 23.3 us -> 0 us
  other arithmetic: 28.2 us -> 5.93 us
  between operations: 15.6 us -> 2.41 us
    pallas_call x0 -> x1, Pallas kernels: none -> 182 us  [local_head(): pl.pallas_call(functools.partial(head_kernel, vocab, tile), out_shape=(ja...]
    reduce_scatter x1 -> x0, waiting for transfers between devices: 144 us -> none  [local_head(): dh = lax.psum_scatter(dh, 'fsdp', scatter_dimension=0, tiled=True)]
    all_gather x2 -> x0, waiting for transfers between devices: 96.2 us -> none  [the longest x1 56.2 us: local_head(): h_all = lax.all_gather(hidden, 'fsdp', axis=0, tiled=True)]
    dot_general x3 -> x0, matrix products: 91.1 us -> none  [the longest x1 32.7 us: local_head(): dh = jnp.dot(dz, weight, preferred_element_type=jnp.float32)]
    all_gather x1 -> x0, blocking collectives: 23.3 us -> none  [local_head(): t_all = lax.all_gather(targets, 'fsdp', axis=0, tiled=True)]
    reduce_sum x3 -> x0, other arithmetic: 22.7 us -> none  [the longest x1 21.4 us: local_head(): row_sum = jnp.sum(jnp.exp(logits - row_max[:, None]), axis=1)]
    mul x0 -> x2, other arithmetic: none -> 5.93 us  [local_head(): return (loss[0, :1] * scale, dh * scale, dw * scale)]
    slice x1 -> x0, other arithmetic: 4.73 us -> none  [local_head(): stats[:, 1] * jnp.exp(stats[:, 0] - all_max)]
  transfers between devices with their start and end apart: 3 -> 0, of which waited for: 3 -> 0; matrix products, arithmetic and copies ran while one was open for 7% -> 0% of each run, Pallas kernels for 0% -> 0%
where the time goes in v3:
time: 192 us
  Pallas kernels  182 us (95%)
  other arithmetic  5.93 us (3%)
  between operations  2.41 us (1%)
    pallas_call x1, Pallas kernels, local_head(): pl.pallas_call(functools.partial(head_kernel, vocab, tile), out_shape=(ja...  182 us
    mul x2, other arithmetic, local_head(): return (loss[0, :1] * scale, dh * scale, dw * scale)  5.93 us

profile of v3, /device:TPU:0, one launch (start us, length us, event | category | flops | bytes accessed | tf_op | source)
XLA Modules:
  0.0 191.6 jit_solution(13122691934309838857)
XLA Ops:
  0.6 181.9 %shard_map.58 = (f32[1,128]{1,0:T(1,128)}, f32[4,512,128]{2,1,0:T(8,128)}, f32[2008,512]{1,0:T(8,128)}) custom-call(bf16[512,512]{1,0:T(8,128)(2,1)} %h_ref.1, s32[1,512]{1,0:T(1,128)} %bitcast.7, bf16[2008,512]{1,0:T(8,128)(2,1)} %w_ref.1), custom_call_target="tpu_custom_call" | custom-call | tf_op jit(solution)/shard_map/pallas_call | solution.py:366
  183.2 1.3 multiply_bitcast_fusion
  184.5 1.3 copy.6
  185.8 4.6 %broadcast_multiply_fusion = f32[2008,512]{1,0:T(8,128)} fusion(f32[2008,512]{1,0:T(8,128)} %get-tuple-element.8), kind=kLoop, calls=%fused_computation | loop fusion | flops 1028096 | bytes 8224768 | tf_op jit(solution)/shard_map/mul | solution.py:384

commit v4 on v3

--- a/solution.py
+++ b/solution.py
@@ -11,33 +11,31 @@
 BF16, F32 = jnp.bfloat16, jnp.float32
 CHUNKS = 4
 COLUMN = ((1, 2, 3), (2, 0, 3), (1, 3, 0), (2, 1, 0))
-DESTS = ((3, 2, 1, 0), (3, 2, 0, 1), (0, 1, 3, 2), (0, 1, 2, 3))
-Y_FIRST = (0, 0, 1, 1)
+DESTS = ((3, 2, 1, 0), (2, 3, 0, 1), (1, 0, 3, 2), (0, 1, 2, 3))
+Y_FIRST = (0, 1, 1, 1)
 SCHEDULE = (
-    ('A', 'own', 0), ('E', 'own', 2), ('I', 'ag', 0, 2), ('A', 'ag', 0, 0), ('E', 'own', 1), ('E', 'ag', 0, 2),
-    ('I', 'own', 1), ('E', 'ag', 2, 0), ('A', 'prep', 2.5), ('I', 'ag', 0, 1), ('A', 'ag', 0, 4), ('I', 'ag', 1, 2),
-    ('E', 'ag', 1, 0), ('A', 'fwd', 0, 0), ('E', 'own', 3), ('I', 'ag', 1, 0), ('I', 'own', 2), ('I', 'ag', 0, 6),
-    ('I', 'ag', 1, 4), ('E', 'ag', 0, 1), ('E', 'ag', 0, 6), ('I', 'ag', 0, 5), ('E', 'ag', 0, 3), ('E', 'ag', 0, 5),
-    ('I', 'ag', 0, 3), ('I', 'ag', 2, 3), ('I', 'ag', 1, 1), ('I', 'ag', 2, 1), ('A', 'fwd', 0, 1), ('E', 'ag', 1, 3),
-    ('E', 'ag', 1, 4), ('I', 'ag', 2, 4), ('E', 'ag', 1, 2), ('I', 'ag', 2, 0), ('I', 'ag', 2, 6), ('A', 'stat', 0),
-    ('I', 'own', 3), ('A', 'bwd', 0, 1, 0), ('E', 'ag', 2, 1), ('E', 'ag', 3, 0), ('A', 'bwd', 0, 1, 1),
-    ('I', 'ag', 1, 6), ('E', 'ag', 1, 1), ('I', 'ag', 1, 3), ('I', 'ag', 1, 5), ('A', 'bwd', 0, 0, 0),
-    ('I', 'ag', 2, 2), ('I', 'ag', 3, 4), ('E', 'ag', 1, 5), ('E', 'ag', 1, 6), ('A', 'fwd', 1, 1), ('I', 'ag', 3, 0),
-    ('E', 'ag', 2, 2), ('A', 'fwd', 1, 0), ('I', 'ag', 3, 3), ('A', 'bwd', 0, 0, 1), ('E', 'hop', 0, 1),
-    ('A', 'stat', 1), ('I', 'ag', 2, 5), ('I', 'ag', 3, 6), ('A', 'bwd', 1, 1, 0), ('E', 'ag', 2, 6),
-    ('E', 'hop', 0, 0), ('A', 'bwd', 1, 1, 1), ('E', 'ag', 2, 3), ('E', 'ag', 2, 5), ('I', 'ag', 3, 1),
-    ('A', 'fwd', 2, 0), ('A', 'bwd', 1, 0, 0), ('I', 'ag', 3, 2), ('E', 'ag', 3, 1), ('E', 'ag', 2, 4),
-    ('I', 'ag', 3, 5), ('I', 'hop', 0, 1), ('I', 'hop', 0, 0), ('A', 'fwd', 2, 1), ('A', 'bwd', 1, 0, 1),
-    ('E', 'ag', 3, 4), ('E', 'ag', 3, 6), ('A', 'stat', 2), ('E', 'hop', 1, 0), ('E', 'ag', 3, 3),
-    ('A', 'bwd', 2, 1, 0), ('E', 'hop', 1, 1), ('A', 'bwd', 2, 1, 1), ('E', 'ag', 3, 5), ('A', 'bwd', 2, 0, 0),
-    ('E', 'ag', 3, 2), ('E', 'hop', 1, 2), ('A', 'fwd', 3, 1), ('I', 'hop', 0, 2), ('A', 'fwd', 3, 0),
-    ('I', 'hop', 1, 0), ('E', 'hop', 0, 2), ('A', 'bwd', 2, 0, 1), ('E', 'hop', 2, 0), ('I', 'hop', 1, 1),
-    ('A', 'stat', 3), ('A', 'bwd', 3, 1, 0), ('A', 'bwd', 3, 0, 0), ('E', 'hop', 2, 1), ('A', 'bwd', 3, 1, 1),
-    ('E', 'hop', 2, 2), ('I', 'hop', 2, 0), ('A', 'bwd', 3, 0, 1), ('A', 'dw_send'), ('I', 'hop', 1, 2),
-    ('I', 'hop', 2, 1), ('A', 'hop', 3, 0), ('I', 'hop', 0, 3), ('I', 'hop', 2, 2), ('I', 'hop', 3, 1),
-    ('I', 'hop', 2, 3), ('I', 'hop', 3, 2), ('E', 'hop', 1, 3), ('E', 'hop', 0, 3), ('E', 'hop', 3, 1),
-    ('E', 'hop', 3, 2), ('E', 'hop', 2, 3), ('E', 'hop', 3, 3), ('A', 'dw_add'), ('I', 'hop', 1, 3),
-    ('I', 'hop', 3, 3),
+    ('A', 'own', 0), ('A', 'prep', 2.5), ('I', 'own', 1), ('I', 'ag', 0, 1), ('E', 'own', 1), ('I', 'ag', 0, 0),
+    ('I', 'ag', 0, 2), ('E', 'ag', 0, 0), ('E', 'ag', 0, 2), ('E', 'ag', 1, 0), ('I', 'own', 3), ('E', 'ag', 0, 3),
+    ('E', 'own', 3), ('I', 'ag', 1, 3), ('E', 'ag', 1, 1), ('A', 'ag', 0, 4), ('I', 'ag', 1, 1), ('A', 'fwd', 0, 0),
+    ('E', 'ag', 1, 3), ('I', 'ag', 1, 4), ('E', 'own', 2), ('I', 'ag', 1, 5), ('E', 'ag', 0, 1), ('E', 'ag', 0, 5),
+    ('E', 'ag', 0, 6), ('I', 'ag', 0, 3), ('I', 'ag', 0, 5), ('I', 'ag', 3, 3), ('I', 'ag', 1, 0), ('E', 'ag', 3, 0),
+    ('I', 'own', 2), ('I', 'ag', 0, 6), ('A', 'fwd', 0, 1), ('E', 'ag', 2, 0), ('I', 'ag', 1, 6), ('E', 'ag', 1, 5),
+    ('E', 'ag', 3, 1), ('A', 'fwd', 1, 0), ('I', 'ag', 1, 2), ('A', 'stat', 0), ('I', 'ag', 3, 4), ('I', 'ag', 3, 5),
+    ('A', 'bwd', 0, 1), ('E', 'ag', 1, 2), ('I', 'ag', 3, 1), ('E', 'ag', 1, 4), ('E', 'ag', 1, 6), ('I', 'ag', 2, 4),
+    ('A', 'fwd', 1, 1), ('I', 'ag', 3, 0), ('I', 'ag', 2, 3), ('I', 'ag', 3, 6), ('A', 'bwd', 0, 0),
+    ('I', 'ag', 2, 0), ('E', 'ag', 3, 3), ('I', 'ag', 2, 6), ('E', 'ag', 3, 2), ('A', 'stat', 1), ('E', 'hop', 0, 0),
+    ('A', 'bwd', 1, 1), ('I', 'ag', 2, 2), ('I', 'ag', 3, 2), ('E', 'ag', 2, 6), ('E', 'hop', 0, 1),
+    ('I', 'ag', 2, 5), ('E', 'ag', 3, 5), ('E', 'ag', 2, 1), ('I', 'hop', 0, 1), ('A', 'bwd', 1, 0),
+    ('E', 'ag', 3, 4), ('E', 'ag', 2, 2), ('I', 'hop', 0, 0), ('I', 'ag', 2, 1), ('E', 'hop', 0, 2),
+    ('E', 'hop', 1, 0), ('E', 'ag', 3, 6), ('E', 'ag', 2, 4), ('A', 'fwd', 3, 0), ('I', 'hop', 0, 2),
+    ('A', 'fwd', 3, 1), ('E', 'ag', 2, 3), ('A', 'fwd', 2, 1), ('E', 'hop', 1, 1), ('A', 'stat', 3),
+    ('A', 'bwd', 3, 1), ('E', 'hop', 1, 2), ('E', 'ag', 2, 5), ('I', 'hop', 0, 3), ('I', 'hop', 1, 0),
+    ('A', 'fwd', 2, 0), ('A', 'bwd', 3, 0), ('E', 'hop', 3, 0), ('A', 'stat', 2), ('E', 'hop', 3, 1),
+    ('I', 'hop', 1, 1), ('A', 'bwd', 2, 1), ('I', 'hop', 3, 1), ('E', 'hop', 3, 2), ('A', 'bwd', 2, 0),
+    ('A', 'dw_send'), ('E', 'hop', 2, 0), ('I', 'hop', 3, 2), ('I', 'hop', 3, 0), ('E', 'hop', 2, 1),
+    ('I', 'hop', 1, 3), ('E', 'hop', 2, 2), ('E', 'hop', 1, 3), ('E', 'hop', 0, 3), ('I', 'hop', 2, 1),
+    ('I', 'hop', 1, 2), ('E', 'hop', 3, 3), ('E', 'hop', 2, 3), ('I', 'hop', 2, 0), ('I', 'hop', 2, 2),
+    ('A', 'dw_add'), ('I', 'hop', 3, 3), ('I', 'hop', 2, 3),
 )
 
 
@@ -47,7 +45,7 @@
 
 
 def head_kernel(vocab, tile, h_ref, t_ref, w_ref, loss_ref, dht_ref, dw_out, x_all, xt_all, t_all, w_all, wt_all, dw, dw_in,
-                far, near, far_in, chain, stats, lse, zt_acc, loss_rows,
+                far, near, far_in, chain, stats, lse, zt_acc, loss_rows, z_even, z_odd,
                 x_recv, x_send, t_recv, t_send, w_sem, st_recv, st_send, ls_recv, ls_send, y_send, y_recv, c_send, c_recv,
                 dw_sem, out_sem):
     tb, d = h_ref.shape
@@ -55,7 +53,7 @@
     vp = w_all.shape[0] // 2
     nt = vp // tile
     groups = tile // 8
-    live = (vocab - (nt - 1) * tile) // 8
+    half_tile = tile // 2
     r = lax.axis_index("fsdp")
     c, chip = r % 2, r // 2
     y, z = chip % 2, chip // 2
@@ -144,11 +142,13 @@
         rows = pl.ds(pl.multiple_of(i * tile, tile), tile)
         return jnp.dot(w_all[rows, :], xt_all[b], preferred_element_type=F32).reshape(groups, 8, tb)
 
-    def mask_pad(vals, i, fill):
-        if live == groups:
+    def mask_pad(vals, i, fill, size):
+        last = vp // size - 1
+        live = (vocab - last * size) // 8
+        if live == size // 8:
             return vals
-        tail = jnp.where((jnp.zeros((groups - live, 8, tb), jnp.int32) + i % nt) == nt - 1, fill, vals[live:])
-        return jnp.concatenate([vals[:live], tail], axis=0)
+        is_last = (jnp.zeros((size // 8 - live, 8, tb), jnp.int32) + i % (last + 1)) == last
+        return jnp.concatenate([vals[:live], jnp.where(is_last, fill, vals[live:])], axis=0)
 
     def place(k, col):
         return 2 * k + y + col * (1 - 2 * y)
@@ -157,14 +157,29 @@
         b = 2 * k + col
         xt_all[b] = x_all[b].reshape(tb, d).T
 
-        def tile_step(i, carry):
+        def logits_into(buf, i):
+            rows = pl.ds(pl.multiple_of(i * half_tile, half_tile), half_tile)
+            buf[...] = jnp.dot(w_all[rows, :], xt_all[b], preferred_element_type=F32)
+
+        def update(buf, i, carry):
             m, s = carry
-            zv = mask_pad(tile_logits(b, i), i, -jnp.inf)
+            zv = mask_pad(buf[...].reshape(half_tile // 8, 8, tb), i, -jnp.inf, half_tile)
             m_new = jnp.maximum(m, jnp.max(zv, axis=0))
-            s = s * jnp.exp(m - m_new) + jnp.sum(jnp.exp(zv - m_new[None]), axis=0)
-            return m_new, s
-
-        m, s = lax.fori_loop(0, 2 * nt, tile_step, (jnp.full((8, tb), -jnp.inf, F32), jnp.zeros((8, tb), F32)))
+            return m_new, s * jnp.exp(m - m_new) + jnp.sum(jnp.exp(zv - m_new[None]), axis=0)
+
+        def pair(j, carry):
+            logits_into(z_odd, 2 * j + 1)
+            carry = update(z_even, 2 * j, carry)
+            logits_into(z_even, 2 * j + 2)
+            return update(z_odd, 2 * j + 1, carry)
+
+        logits_into(z_even, 0)
+        pairs = 2 * vp // (2 * half_tile)
+        carry = (jnp.full((8, tb), -jnp.inf, F32), jnp.zeros((8, tb), F32))
+        carry = lax.fori_loop(0, pairs - 1, pair, carry)
+        logits_into(z_odd, 2 * pairs - 1)
+        carry = update(z_even, 2 * pairs - 2, carry)
+        m, s = update(z_odd, 2 * pairs - 1, carry)
         m1 = jnp.max(m, axis=0, keepdims=True)
         s1 = jnp.sum(s * jnp.exp(m - m1), axis=0, keepdims=True)
         p = place(k, col)
@@ -183,24 +198,23 @@
     iota8 = lax.broadcasted_iota(jnp.int32, (8, tb), 0)
     group8 = lax.broadcasted_iota(jnp.int32, (groups, 8, tb), 0) * 8
 
-    def backward(k, col, half):
+    def backward(k, col):
         b = 2 * k + col
         acc = far if col else near
         phys = y + col * (1 - 2 * y)
-        if half == 0:
-            acc[k] = jnp.zeros((4, d, tc), F32)
+        acc[k] = jnp.zeros((4, d, tc), F32)
         norm = jnp.broadcast_to(lse[place(k, col)], (8, tb))[None]
         ids = jnp.concatenate([t_all[2 * q + phys][:, k * tc:(k + 1) * tc] for q in range(4)], axis=1)
-        rel = ids - vocab * (mate if half else r)
-        rel = jnp.where((rel >= 0) & (rel < vocab), rel, -2 * vp)
-        rel8 = jnp.broadcast_to(rel, (8, tb)) - iota8
 
         def tile_step(i, _):
+            slot = i // nt
+            rel = ids - vocab * (r * (1 - slot) + mate * slot)
+            rel = jnp.where((rel >= 0) & (rel < vocab), rel - (i % nt) * tile, -2 * vp)
             rows = pl.ds(pl.multiple_of(i * tile, tile), tile)
             zv = tile_logits(b, i)
-            hit = (rel8 - (i - half * nt) * tile)[None] == group8
+            hit = (jnp.broadcast_to(rel, (8, tb)) - iota8)[None] == group8
             zt_acc[...] += jnp.sum(jnp.where(hit, zv, 0.0), axis=0)
-            dz = mask_pad(jnp.exp(zv - norm) - jnp.where(hit, 1.0, 0.0), i, 0.0)
+            dz = mask_pad(jnp.exp(zv - norm) - jnp.where(hit, 1.0, 0.0), i, 0.0, tile)
             dz = dz.reshape(tile, tb).astype(BF16)
             part = jnp.dot(wt_all[i], dz, preferred_element_type=F32)
             for q in range(4):
@@ -208,8 +222,8 @@
             dw[rows, :] += jnp.dot(dz, x_all[b].reshape(tb, d), preferred_element_type=F32)
             return 0
 
-        lax.fori_loop(half * nt, (half + 1) * nt, tile_step, 0)
-        if col == 1 and half == 1:
+        lax.fori_loop(0, 2 * nt, tile_step, 0)
+        if col:
             for j in range(4):
                 y_copy(k, dest(j)).start()
 
@@ -351,7 +365,7 @@
     dw_store.wait()
 
 
-def solution(mesh, tile=512):
+def solution(mesh, tile=1024):
     groups = mesh.shape["fsdp"]
     tok_spec = P(("dp", "fsdp"), None)
 
@@ -374,6 +388,7 @@
                 vmem((2 * vp, d), F32), vmem((vp, d), F32),
                 vmem((CHUNKS, 4, d, tc), F32), vmem((CHUNKS, 4, d, tc), F32), vmem((CHUNKS, 4, d, tc), F32), vmem((CHUNKS, 5, d, tc), F32),
                 vmem((8, 8, 2, tb), F32), vmem((8, 1, tb), F32), vmem((8, tb), F32), vmem((16, 1, tb), F32),
+                vmem((tile // 2, tb), F32), vmem((tile // 2, tb), F32),
                 dma((8, 4)), dma((3, CHUNKS, 8)), dma, dma, dma((2,)), dma((CHUNKS,)), dma, dma, dma,
                 dma((CHUNKS, 4)), dma((CHUNKS, 4)), dma((CHUNKS, 3)), dma((CHUNKS, 5)), dma((2,)), dma((CHUNKS + 1,)),
             ],

time: 192 us -> 181 us (0.943)
  Pallas kernels: 182 us -> 172 us
    pallas_call x1, Pallas kernels: 182 us -> 172 us  [local_head(): pl.pallas_call(functools.partial(head_kernel, vocab, tile), out_shape=(ja...]
where the time goes in v4:
time: 181 us
  Pallas kernels  172 us (95%)
  other arithmetic  5.93 us (3%)
  between operations  2.41 us (1%)
    pallas_call x1, Pallas kernels, local_head(): pl.pallas_call(functools.partial(head_kernel, vocab, tile), out_shape=(ja...  172 us
    mul x2, other arithmetic, local_head(): return (loss[0, :1] * scale, dh * scale, dw * scale)  5.93 us

profile of v4, /device:TPU:0, one launch (start us, length us, event | category | flops | bytes accessed | tf_op | source)
XLA Modules:
  0.0 181.2 jit_solution(12818224250372311665)
XLA Ops:
  0.6 171.5 %shard_map.58 = (f32[1,128]{1,0:T(1,128)}, f32[4,512,128]{2,1,0:T(8,128)}, f32[2008,512]{1,0:T(8,128)}) custom-call(bf16[512,512]{1,0:T(8,128)(2,1)} %h_ref.1, s32[1,512]{1,0:T(1,128)} %bitcast.7, bf16[2008,512]{1,0:T(8,128)(2,1)} %w_ref.1), custom_call_target="tpu_custom_call" | custom-call | tf_op jit(solution)/shard_map/pallas_call | solution.py:380
  172.8 1.3 multiply_bitcast_fusion
  174.1 1.3 copy.6
  175.4 4.6 %broadcast_multiply_fusion = f32[2008,512]{1,0:T(8,128)} fusion(f32[2008,512]{1,0:T(8,128)} %get-tuple-element.8), kind=kLoop, calls=%fused_computation | loop fusion | flops 1028096 | bytes 8224768 | tf_op jit(solution)/shard_map/mul | solution.py:399

commit v5 on v4

--- a/solution.py
+++ b/solution.py
@@ -11,31 +11,36 @@
 BF16, F32 = jnp.bfloat16, jnp.float32
 CHUNKS = 4
 COLUMN = ((1, 2, 3), (2, 0, 3), (1, 3, 0), (2, 1, 0))
-DESTS = ((3, 2, 1, 0), (2, 3, 0, 1), (1, 0, 3, 2), (0, 1, 2, 3))
-Y_FIRST = (0, 1, 1, 1)
+DESTS = ((3, 2, 1, 0), (3, 0, 2, 1), (0, 3, 1, 2), (0, 1, 2, 3))
+Y_FIRST = (0, 0, 1, 1)
 SCHEDULE = (
-    ('A', 'own', 0), ('A', 'prep', 2.5), ('I', 'own', 1), ('I', 'ag', 0, 1), ('E', 'own', 1), ('I', 'ag', 0, 0),
-    ('I', 'ag', 0, 2), ('E', 'ag', 0, 0), ('E', 'ag', 0, 2), ('E', 'ag', 1, 0), ('I', 'own', 3), ('E', 'ag', 0, 3),
-    ('E', 'own', 3), ('I', 'ag', 1, 3), ('E', 'ag', 1, 1), ('A', 'ag', 0, 4), ('I', 'ag', 1, 1), ('A', 'fwd', 0, 0),
-    ('E', 'ag', 1, 3), ('I', 'ag', 1, 4), ('E', 'own', 2), ('I', 'ag', 1, 5), ('E', 'ag', 0, 1), ('E', 'ag', 0, 5),
-    ('E', 'ag', 0, 6), ('I', 'ag', 0, 3), ('I', 'ag', 0, 5), ('I', 'ag', 3, 3), ('I', 'ag', 1, 0), ('E', 'ag', 3, 0),
-    ('I', 'own', 2), ('I', 'ag', 0, 6), ('A', 'fwd', 0, 1), ('E', 'ag', 2, 0), ('I', 'ag', 1, 6), ('E', 'ag', 1, 5),
-    ('E', 'ag', 3, 1), ('A', 'fwd', 1, 0), ('I', 'ag', 1, 2), ('A', 'stat', 0), ('I', 'ag', 3, 4), ('I', 'ag', 3, 5),
-    ('A', 'bwd', 0, 1), ('E', 'ag', 1, 2), ('I', 'ag', 3, 1), ('E', 'ag', 1, 4), ('E', 'ag', 1, 6), ('I', 'ag', 2, 4),
-    ('A', 'fwd', 1, 1), ('I', 'ag', 3, 0), ('I', 'ag', 2, 3), ('I', 'ag', 3, 6), ('A', 'bwd', 0, 0),
-    ('I', 'ag', 2, 0), ('E', 'ag', 3, 3), ('I', 'ag', 2, 6), ('E', 'ag', 3, 2), ('A', 'stat', 1), ('E', 'hop', 0, 0),
-    ('A', 'bwd', 1, 1), ('I', 'ag', 2, 2), ('I', 'ag', 3, 2), ('E', 'ag', 2, 6), ('E', 'hop', 0, 1),
-    ('I', 'ag', 2, 5), ('E', 'ag', 3, 5), ('E', 'ag', 2, 1), ('I', 'hop', 0, 1), ('A', 'bwd', 1, 0),
-    ('E', 'ag', 3, 4), ('E', 'ag', 2, 2), ('I', 'hop', 0, 0), ('I', 'ag', 2, 1), ('E', 'hop', 0, 2),
-    ('E', 'hop', 1, 0), ('E', 'ag', 3, 6), ('E', 'ag', 2, 4), ('A', 'fwd', 3, 0), ('I', 'hop', 0, 2),
-    ('A', 'fwd', 3, 1), ('E', 'ag', 2, 3), ('A', 'fwd', 2, 1), ('E', 'hop', 1, 1), ('A', 'stat', 3),
-    ('A', 'bwd', 3, 1), ('E', 'hop', 1, 2), ('E', 'ag', 2, 5), ('I', 'hop', 0, 3), ('I', 'hop', 1, 0),
-    ('A', 'fwd', 2, 0), ('A', 'bwd', 3, 0), ('E', 'hop', 3, 0), ('A', 'stat', 2), ('E', 'hop', 3, 1),
-    ('I', 'hop', 1, 1), ('A', 'bwd', 2, 1), ('I', 'hop', 3, 1), ('E', 'hop', 3, 2), ('A', 'bwd', 2, 0),
-    ('A', 'dw_send'), ('E', 'hop', 2, 0), ('I', 'hop', 3, 2), ('I', 'hop', 3, 0), ('E', 'hop', 2, 1),
-    ('I', 'hop', 1, 3), ('E', 'hop', 2, 2), ('E', 'hop', 1, 3), ('E', 'hop', 0, 3), ('I', 'hop', 2, 1),
-    ('I', 'hop', 1, 2), ('E', 'hop', 3, 3), ('E', 'hop', 2, 3), ('I', 'hop', 2, 0), ('I', 'hop', 2, 2),
-    ('A', 'dw_add'), ('I', 'hop', 3, 3), ('I', 'hop', 2, 3),
+    ('I', 'own', 0), ('I', 'own', 2), ('E', 'own', 0), ('I', 'ag', 0, 2), ('E', 'own', 1), ('E', 'own', 2),
+    ('E', 'ag', 1, 1), ('E', 'ag', 2, 1), ('I', 'ag', 0, 0), ('E', 'own', 3), ('E', 'ag', 0, 0), ('A', 'prep', 2.5),
+    ('I', 'own', 1), ('I', 'ag', 0, 4), ('E', 'ag', 2, 0), ('I', 'ag', 0, 1), ('E', 'ag', 0, 3), ('I', 'ag', 2, 3),
+    ('E', 'ag', 0, 4), ('I', 'ag', 1, 2), ('E', 'ag', 0, 2), ('A', 'fwd', 0, 0), ('I', 'ag', 2, 1), ('E', 'ag', 3, 0),
+    ('E', 'ag', 2, 3), ('E', 'ag', 1, 0), ('I', 'ag', 2, 5), ('I', 'ag', 0, 3), ('I', 'ag', 1, 4), ('I', 'ag', 1, 0),
+    ('I', 'ag', 2, 4), ('I', 'ag', 0, 5), ('E', 'ag', 2, 5), ('A', 'fwd', 2, 0), ('E', 'ag', 0, 5), ('E', 'ag', 0, 1),
+    ('I', 'ag', 2, 0), ('I', 'ag', 1, 1), ('I', 'ag', 1, 5), ('A', 'ag', 0, 6), ('E', 'ag', 1, 4), ('I', 'ag', 3, 4),
+    ('A', 'fwd', 0, 1), ('I', 'ag', 2, 6), ('I', 'own', 3), ('E', 'ag', 1, 2), ('A', 'fwd', 1, 0), ('A', 'stat', 0),
+    ('E', 'ag', 1, 6), ('E', 'ag', 1, 5), ('A', 'ag', 1, 3), ('I', 'ag', 2, 2), ('I', 'ag', 1, 6), ('A', 'fwd', 1, 1),
+    ('A', 'bwd', 0, 1), ('I', 'ag', 3, 6), ('A', 'stat', 1), ('E', 'ag', 2, 4), ('I', 'ys', 0, 1), ('E', 'ag', 2, 6),
+    ('E', 'ag', 2, 2), ('I', 'ag', 3, 1), ('I', 'ag', 3, 3), ('E', 'ys', 0, 1), ('A', 'fwd', 2, 1),
+    ('A', 'bwd', 1, 1), ('I', 'ys', 0, 0), ('A', 'stat', 2), ('E', 'ys', 1, 0), ('E', 'ys', 1, 1), ('E', 'ys', 0, 2),
+    ('I', 'ag', 3, 5), ('I', 'ys', 1, 1), ('I', 'ag', 3, 0), ('A', 'bwd', 2, 1), ('E', 'ys', 0, 0), ('I', 'ys', 2, 1),
+    ('I', 'ys', 1, 0), ('E', 'ys', 2, 0), ('E', 'ag', 3, 2), ('E', 'ys', 0, 3), ('I', 'ys', 1, 2), ('I', 'ys', 2, 0),
+    ('A', 'bwd', 1, 0), ('E', 'ag', 3, 5), ('I', 'ag', 3, 2), ('E', 'hop', 1, 1), ('E', 'hop', 1, 0),
+    ('A', 'bwd', 0, 0), ('E', 'ag', 3, 4), ('E', 'ag', 3, 6), ('E', 'hop', 0, 1), ('A', 'fwd', 3, 1),
+    ('E', 'ag', 3, 3), ('E', 'ys', 2, 1), ('E', 'ag', 3, 1), ('I', 'ys', 0, 2), ('A', 'fwd', 3, 0), ('I', 'ys', 2, 2),
+    ('E', 'hop', 0, 0), ('I', 'hop', 1, 0), ('E', 'ys', 1, 2), ('E', 'ys', 2, 2), ('E', 'hop', 0, 2),
+    ('A', 'bwd', 2, 0), ('I', 'hop', 0, 0), ('I', 'ys', 1, 3), ('A', 'stat', 3), ('E', 'hop', 2, 0),
+    ('E', 'hop', 2, 1), ('I', 'hop', 1, 2), ('I', 'ys', 2, 3), ('E', 'ys', 1, 3), ('I', 'hop', 1, 1),
+    ('A', 'bwd', 3, 1), ('A', 'ys', 3, 0), ('I', 'ys', 3, 2), ('I', 'ys', 3, 1), ('I', 'hop', 0, 2),
+    ('I', 'ys', 0, 3), ('I', 'ys', 3, 3), ('I', 'hop', 2, 0), ('E', 'ys', 3, 1), ('I', 'hop', 0, 1),
+    ('E', 'ys', 2, 3), ('I', 'hop', 2, 2), ('E', 'ys', 3, 2), ('E', 'hop', 2, 2), ('A', 'bwd', 3, 0),
+    ('A', 'dw_send'), ('I', 'hop', 2, 1), ('A', 'hop', 3, 0), ('E', 'hop', 1, 3), ('E', 'hop', 3, 1),
+    ('E', 'hop', 1, 2), ('I', 'hop', 3, 2), ('I', 'hop', 2, 3), ('I', 'hop', 3, 1), ('I', 'hop', 0, 3),
+    ('E', 'hop', 2, 3), ('I', 'hop', 1, 3), ('E', 'hop', 0, 3), ('E', 'ys', 3, 3), ('E', 'hop', 3, 2),
+    ('A', 'dw_add'), ('A', 'hop', 3, 3),
 )
 
 
@@ -223,9 +228,6 @@
             return 0
 
         lax.fori_loop(0, 2 * nt, tile_step, 0)
-        if col:
-            for j in range(4):
-                y_copy(k, dest(j)).start()
 
     def dest(j):
         return pick(z, [DESTS[q][j] for q in range(4)])
@@ -328,6 +330,8 @@
                 gather(*args)
             elif kind == "hop":
                 hop(*args)
+            elif kind == "ys":
+                y_copy(args[0], dest(args[1])).start()
             elif kind == "prep":
                 prepare()
             elif kind == "fwd":

time: 181 us -> 167 us (0.923)
  Pallas kernels: 172 us -> 157 us
    pallas_call x1, Pallas kernels: 172 us -> 157 us  [local_head(): pl.pallas_call(functools.partial(head_kernel, vocab, tile), out_shape=(ja...]
where the time goes in v5:
time: 167 us
  Pallas kernels  157 us (94%)
  other arithmetic  5.93 us (4%)
  between operations  2.41 us (1%)
    pallas_call x1, Pallas kernels, local_head(): pl.pallas_call(functools.partial(head_kernel, vocab, tile), out_shape=(ja...  157 us
    mul x2, other arithmetic, local_head(): return (loss[0, :1] * scale, dh * scale, dw * scale)  5.93 us

profile of v5, /device:TPU:0, one launch (start us, length us, event | category | flops | bytes accessed | tf_op | source)
XLA Modules:
  0.0 166.9 jit_solution(2025628992794453011)
XLA Ops:
  0.6 157.2 %shard_map.58 = (f32[1,128]{1,0:T(1,128)}, f32[4,512,128]{2,1,0:T(8,128)}, f32[2008,512]{1,0:T(8,128)}) custom-call(bf16[512,512]{1,0:T(8,128)(2,1)} %h_ref.1, s32[1,512]{1,0:T(1,128)} %bitcast.7, bf16[2008,512]{1,0:T(8,128)(2,1)} %w_ref.1), custom_call_target="tpu_custom_call" | custom-call | tf_op jit(solution)/shard_map/pallas_call | solution.py:384
  158.5 1.3 multiply_bitcast_fusion
  159.8 1.3 copy.6
  161.1 4.6 %broadcast_multiply_fusion = f32[2008,512]{1,0:T(8,128)} fusion(f32[2008,512]{1,0:T(8,128)} %get-tuple-element.8), kind=kLoop, calls=%fused_computation | loop fusion | flops 1028096 | bytes 8224768 | tf_op jit(solution)/shard_map/mul | solution.py:403

commit v6 on v4

--- a/solution.py
+++ b/solution.py
@@ -11,31 +11,35 @@
 BF16, F32 = jnp.bfloat16, jnp.float32
 CHUNKS = 4
 COLUMN = ((1, 2, 3), (2, 0, 3), (1, 3, 0), (2, 1, 0))
-DESTS = ((3, 2, 1, 0), (2, 3, 0, 1), (1, 0, 3, 2), (0, 1, 2, 3))
+DESTS = ((3, 2, 1, 0), (3, 2, 0, 1), (0, 1, 3, 2), (0, 1, 2, 3))
 Y_FIRST = (0, 1, 1, 1)
 SCHEDULE = (
-    ('A', 'own', 0), ('A', 'prep', 2.5), ('I', 'own', 1), ('I', 'ag', 0, 1), ('E', 'own', 1), ('I', 'ag', 0, 0),
-    ('I', 'ag', 0, 2), ('E', 'ag', 0, 0), ('E', 'ag', 0, 2), ('E', 'ag', 1, 0), ('I', 'own', 3), ('E', 'ag', 0, 3),
-    ('E', 'own', 3), ('I', 'ag', 1, 3), ('E', 'ag', 1, 1), ('A', 'ag', 0, 4), ('I', 'ag', 1, 1), ('A', 'fwd', 0, 0),
-    ('E', 'ag', 1, 3), ('I', 'ag', 1, 4), ('E', 'own', 2), ('I', 'ag', 1, 5), ('E', 'ag', 0, 1), ('E', 'ag', 0, 5),
-    ('E', 'ag', 0, 6), ('I', 'ag', 0, 3), ('I', 'ag', 0, 5), ('I', 'ag', 3, 3), ('I', 'ag', 1, 0), ('E', 'ag', 3, 0),
-    ('I', 'own', 2), ('I', 'ag', 0, 6), ('A', 'fwd', 0, 1), ('E', 'ag', 2, 0), ('I', 'ag', 1, 6), ('E', 'ag', 1, 5),
-    ('E', 'ag', 3, 1), ('A', 'fwd', 1, 0), ('I', 'ag', 1, 2), ('A', 'stat', 0), ('I', 'ag', 3, 4), ('I', 'ag', 3, 5),
-    ('A', 'bwd', 0, 1), ('E', 'ag', 1, 2), ('I', 'ag', 3, 1), ('E', 'ag', 1, 4), ('E', 'ag', 1, 6), ('I', 'ag', 2, 4),
-    ('A', 'fwd', 1, 1), ('I', 'ag', 3, 0), ('I', 'ag', 2, 3), ('I', 'ag', 3, 6), ('A', 'bwd', 0, 0),
-    ('I', 'ag', 2, 0), ('E', 'ag', 3, 3), ('I', 'ag', 2, 6), ('E', 'ag', 3, 2), ('A', 'stat', 1), ('E', 'hop', 0, 0),
-    ('A', 'bwd', 1, 1), ('I', 'ag', 2, 2), ('I', 'ag', 3, 2), ('E', 'ag', 2, 6), ('E', 'hop', 0, 1),
-    ('I', 'ag', 2, 5), ('E', 'ag', 3, 5), ('E', 'ag', 2, 1), ('I', 'hop', 0, 1), ('A', 'bwd', 1, 0),
-    ('E', 'ag', 3, 4), ('E', 'ag', 2, 2), ('I', 'hop', 0, 0), ('I', 'ag', 2, 1), ('E', 'hop', 0, 2),
-    ('E', 'hop', 1, 0), ('E', 'ag', 3, 6), ('E', 'ag', 2, 4), ('A', 'fwd', 3, 0), ('I', 'hop', 0, 2),
-    ('A', 'fwd', 3, 1), ('E', 'ag', 2, 3), ('A', 'fwd', 2, 1), ('E', 'hop', 1, 1), ('A', 'stat', 3),
-    ('A', 'bwd', 3, 1), ('E', 'hop', 1, 2), ('E', 'ag', 2, 5), ('I', 'hop', 0, 3), ('I', 'hop', 1, 0),
-    ('A', 'fwd', 2, 0), ('A', 'bwd', 3, 0), ('E', 'hop', 3, 0), ('A', 'stat', 2), ('E', 'hop', 3, 1),
-    ('I', 'hop', 1, 1), ('A', 'bwd', 2, 1), ('I', 'hop', 3, 1), ('E', 'hop', 3, 2), ('A', 'bwd', 2, 0),
-    ('A', 'dw_send'), ('E', 'hop', 2, 0), ('I', 'hop', 3, 2), ('I', 'hop', 3, 0), ('E', 'hop', 2, 1),
-    ('I', 'hop', 1, 3), ('E', 'hop', 2, 2), ('E', 'hop', 1, 3), ('E', 'hop', 0, 3), ('I', 'hop', 2, 1),
-    ('I', 'hop', 1, 2), ('E', 'hop', 3, 3), ('E', 'hop', 2, 3), ('I', 'hop', 2, 0), ('I', 'hop', 2, 2),
-    ('A', 'dw_add'), ('I', 'hop', 3, 3), ('I', 'hop', 2, 3),
+    ('A', 'own', 0), ('A', 'prep', 2.5), ('E', 'own', 1), ('E', 'own', 2), ('E', 'ag', 0, 0), ('I', 'own', 1),
+    ('E', 'ag', 1, 0), ('E', 'ag', 2, 0), ('A', 'ag', 0, 2), ('E', 'ag', 0, 3), ('E', 'ag', 1, 2), ('E', 'ag', 0, 4),
+    ('I', 'ag', 0, 1), ('I', 'ag', 0, 0), ('I', 'ag', 1, 3), ('I', 'ag', 1, 0), ('E', 'own', 3), ('E', 'ag', 0, 1),
+    ('I', 'ag', 0, 4), ('I', 'ag', 0, 5), ('A', 'fwd', 0, 0), ('I', 'ag', 2, 3), ('I', 'ag', 1, 1), ('I', 'ag', 1, 4),
+    ('I', 'ag', 0, 6), ('I', 'ag', 0, 3), ('E', 'ag', 0, 5), ('I', 'ag', 1, 5), ('E', 'ag', 1, 1), ('E', 'ag', 0, 6),
+    ('I', 'ag', 2, 4), ('A', 'fwd', 0, 1), ('E', 'ag', 1, 5), ('I', 'ag', 1, 2), ('I', 'ag', 1, 6), ('I', 'own', 2),
+    ('I', 'own', 3), ('E', 'ag', 1, 3), ('A', 'fwd', 1, 0), ('E', 'ag', 1, 4), ('E', 'ag', 1, 6), ('I', 'ag', 2, 0),
+    ('A', 'fwd', 1, 1), ('A', 'stat', 0), ('I', 'ag', 2, 1), ('A', 'bwd', 0, 1), ('E', 'ys', 0, 0), ('I', 'ys', 0, 1),
+    ('I', 'ag', 3, 0), ('I', 'ag', 2, 2), ('I', 'ag', 2, 5), ('A', 'stat', 1), ('E', 'ys', 0, 2), ('E', 'ag', 2, 3),
+    ('I', 'ag', 3, 3), ('A', 'bwd', 0, 0), ('I', 'ys', 0, 2), ('I', 'ys', 0, 0), ('E', 'ag', 2, 1), ('I', 'ag', 2, 6),
+    ('E', 'ag', 2, 2), ('E', 'ag', 3, 0), ('E', 'hop', 0, 0), ('E', 'ag', 2, 5), ('E', 'ys', 0, 1),
+    ('A', 'bwd', 1, 1), ('E', 'ag', 2, 6), ('E', 'hop', 0, 2), ('A', 'ys', 1, 1), ('I', 'ag', 3, 5),
+    ('A', 'fwd', 2, 0), ('E', 'ag', 2, 4), ('E', 'hop', 0, 1), ('I', 'ag', 3, 4), ('A', 'fwd', 2, 1),
+    ('E', 'ag', 3, 5), ('E', 'ys', 1, 0), ('I', 'ag', 3, 1), ('I', 'ys', 1, 0), ('A', 'bwd', 1, 0), ('E', 'ag', 3, 2),
+    ('I', 'ys', 1, 3), ('E', 'hop', 1, 0), ('E', 'ys', 1, 3), ('I', 'ag', 3, 6), ('I', 'ag', 3, 2),
+    ('I', 'hop', 0, 0), ('A', 'stat', 2), ('E', 'ys', 1, 2), ('I', 'ys', 0, 3), ('E', 'ag', 3, 3), ('A', 'bwd', 2, 1),
+    ('E', 'ys', 2, 0), ('E', 'ag', 3, 1), ('E', 'ag', 3, 6), ('E', 'hop', 1, 1), ('I', 'ys', 1, 2),
+    ('I', 'hop', 0, 1), ('E', 'ag', 3, 4), ('A', 'fwd', 3, 1), ('I', 'ys', 2, 0), ('A', 'fwd', 3, 0),
+    ('I', 'hop', 0, 2), ('A', 'ys', 2, 1), ('I', 'hop', 1, 0), ('A', 'ys', 2, 2), ('E', 'hop', 1, 2),
+    ('A', 'bwd', 2, 0), ('E', 'hop', 2, 1), ('I', 'hop', 0, 3), ('E', 'hop', 2, 0), ('A', 'stat', 3),
+    ('I', 'hop', 1, 2), ('I', 'hop', 1, 1), ('E', 'ys', 0, 3), ('A', 'bwd', 3, 1), ('I', 'ys', 3, 0),
+    ('I', 'hop', 2, 1), ('I', 'hop', 2, 0), ('I', 'ys', 3, 2), ('E', 'hop', 2, 2), ('I', 'ys', 3, 1),
+    ('E', 'ys', 3, 0), ('E', 'ys', 3, 1), ('E', 'ys', 3, 2), ('A', 'bwd', 3, 0), ('A', 'dw_send'), ('E', 'hop', 3, 0),
+    ('I', 'hop', 2, 2), ('I', 'hop', 3, 0), ('I', 'ys', 2, 3), ('E', 'hop', 0, 3), ('E', 'hop', 3, 1),
+    ('I', 'ys', 3, 3), ('A', 'hop', 1, 3), ('I', 'hop', 3, 1), ('I', 'hop', 3, 2), ('I', 'hop', 2, 3),
+    ('E', 'ys', 3, 3), ('E', 'hop', 3, 2), ('E', 'ys', 2, 3), ('E', 'hop', 2, 3), ('A', 'dw_add'), ('A', 'hop', 3, 3),
 )
 
 
@@ -223,9 +227,6 @@
             return 0
 
         lax.fori_loop(0, 2 * nt, tile_step, 0)
-        if col:
-            for j in range(4):
-                y_copy(k, dest(j)).start()
 
     def dest(j):
         return pick(z, [DESTS[q][j] for q in range(4)])
@@ -328,6 +329,8 @@
                 gather(*args)
             elif kind == "hop":
                 hop(*args)
+            elif kind == "ys":
+                y_copy(args[0], dest(args[1])).start()
             elif kind == "prep":
                 prepare()
             elif kind == "fwd":
@@ -363,6 +366,31 @@
         out_copy(k).wait()
     dw_copy.wait_send()
     dw_store.wait()
+
+
+def finish_kernel(scale, dht_ref, dw_ref, dh_out, dw_out, dht, dh, dw, in_sem, out_sem):
+    chunks, d, tc = dht.shape
+    vocab = dw.shape[0]
+    step = -(-vocab // 64) * 8
+    spans = [pl.ds(lo, min(step, vocab - lo)) for lo in range(0, vocab, step)]
+    loads = [pltpu.make_async_copy(dw_ref.at[s], dw.at[s], in_sem.at[n]) for n, s in enumerate(spans)]
+    loads += [pltpu.make_async_copy(dht_ref.at[k], dht.at[k], in_sem.at[8 + k]) for k in range(chunks)]
+    for load in loads:
+        load.start()
+    stores = []
+    for n, s in enumerate(spans):
+        loads[n].wait()
+        dw[s, :] = dw[s, :] * scale
+        stores.append(pltpu.make_async_copy(dw.at[s], dw_out.at[s], out_sem.at[n]))
+        stores[-1].start()
+    for k in range(chunks):
+        loads[len(spans) + k].wait()
+        rows = pl.ds(k * tc, tc)
+        dh[rows, :] = dht[k].T * scale
+        stores.append(pltpu.make_async_copy(dh.at[rows], dh_out.at[rows], out_sem.at[8 + k]))
+        stores[-1].start()
+    for store in stores:
+        store.wait()
 
 
 def solution(mesh, tile=1024):
@@ -395,7 +423,13 @@
             compiler_params=pltpu.CompilerParams(collective_id=0, has_side_effects=True, vmem_limit_bytes=66_000_000),
         )(hidden, targets.reshape(1, tb), weight)
         scale = 1.0 / (tb * groups)
-        dh = dht.transpose(0, 2, 1).reshape(tb, d)
-        return loss[0, :1] * scale, dh * scale, dw * scale
+        dh, dw = pl.pallas_call(
+            functools.partial(finish_kernel, scale),
+            out_shape=(jax.ShapeDtypeStruct((tb, d), F32), jax.ShapeDtypeStruct((vocab, d), F32)),
+            in_specs=[pl.BlockSpec(memory_space=pl.ANY)] * 2,
+            out_specs=(pl.BlockSpec(memory_space=pl.ANY), pl.BlockSpec(memory_space=pl.ANY)),
+            scratch_shapes=[vmem((CHUNKS, d, tc), F32), vmem((tb, d), F32), vmem((vocab, d), F32), dma((8 + CHUNKS,)), dma((8 + CHUNKS,))],
+        )(dht, dw)
+        return loss[0, :1] * scale, dh, dw
 
     return jax.shard_map(local_head, mesh=mesh, in_specs=(tok_spec, P(("dp", "fsdp")), P("fsdp", None)), out_specs=(P("dp"), tok_spec, tok_spec), check_vma=False)

time: 181 us -> 159 us (0.88)
  Pallas kernels: 172 us -> 156 us
  other arithmetic: 5.93 us -> 0 us
    pallas_call x1, Pallas kernels: 172 us -> 152 us  [local_head(): pl.pallas_call(functools.partial(head_kernel, vocab, tile), out_shape=(ja...]
    mul x2 -> x0, other arithmetic: 5.93 us -> none  [local_head(): return (loss[0, :1] * scale, dh * scale, dw * scale)]
    pallas_call x0 -> x1, Pallas kernels: none -> 4.61 us  [local_head(): pl.pallas_call(functools.partial(finish_kernel, scale), out_shape=(jax.Sh...]
where the time goes in v6:
time: 159 us
  Pallas kernels  156 us (98%)
  between operations  2.41 us (2%)
    pallas_call x1, Pallas kernels, local_head(): pl.pallas_call(functools.partial(head_kernel, vocab, tile), out_shape=(ja...  152 us
    pallas_call x1, Pallas kernels, local_head(): pl.pallas_call(functools.partial(finish_kernel, scale), out_shape=(jax.Sh...  4.61 us

profile of v6, /device:TPU:0, one launch (start us, length us, event | category | flops | bytes accessed | tf_op | source)
XLA Modules:
  0.0 158.8 jit_solution(1529052571270716547)
XLA Ops:
  0.6 151.8 %shard_map.58 = (f32[1,128]{1,0:T(1,128)}, f32[4,512,128]{2,1,0:T(8,128)}, f32[2008,512]{1,0:T(8,128)}) custom-call(bf16[512,512]{1,0:T(8,128)(2,1)} %h_ref.1, s32[1,512]{1,0:T(1,128)} %bitcast.3, bf16[2008,512]{1,0:T(8,128)(2,1)} %w_ref.1), custom_call_target="tpu_custom_call" | custom-call | tf_op jit(solution)/shard_map/pallas_call | solution.py:408
  153.1 4.6 %shard_map.59 = (f32[512,512]{1,0:T(8,128)}, f32[2008,512]{1,0:T(8,128)}) custom-call(f32[4,512,128]{2,1,0:T(8,128)} %get-tuple-element.9.dht_ref, f32[2008,512]{1,0:T(8,128)} %get-tuple-element.10.dw_ref), custom_call_target="tpu_custom_call" | custom-call | tf_op jit(solution)/shard_map/pallas_call | solution.py:426

commit v7 on v6

--- a/solution.py
+++ b/solution.py
@@ -87,7 +87,6 @@
         dw[pl.ds(pl.multiple_of(i * tile, tile), tile), :] = jnp.zeros((tile, d), F32)
         return 0
 
-    lax.fori_loop(0, nt, transpose_w, 0)
     pl.semaphore_wait(barrier, 15)
 
     w_copy = remote(w_all.at[pl.ds(0, vp)], w_all.at[pl.ds(vp, vp)], w_sem.at[0], w_sem.at[1], mate)
@@ -101,8 +100,7 @@
         w_copy.start()
         lax.fori_loop(0, 2 * nt, zero_dw, 0)
         zt_acc[...] = jnp.zeros_like(zt_acc)
-        w_copy.wait()
-        lax.fori_loop(nt, 2 * nt, transpose_w, 0)
+        lax.fori_loop(0, nt, transpose_w, 0)
 
     def x_copy(k, col, zs, way, slot):
         dev = (across, left, right)[way]
@@ -317,8 +315,13 @@
     def start(copy):
         copy.start()
 
-    first_backward = [e[1] for e in SCHEDULE].index("bwd")
+    kinds = [e[1] for e in SCHEDULE]
+    first_forward, first_stat, first_backward = kinds.index("fwd"), kinds.index("stat"), kinds.index("bwd")
     for n, (who, kind, *args) in enumerate(SCHEDULE):
+        if n == first_forward:
+            w_copy.wait()
+        if n == first_stat:
+            lax.fori_loop(nt, 2 * nt, transpose_w, 0)
         if n == first_backward:
             drain(t_all.at[pl.ds(0, 7)], t_recv)
 

time: 159 us -> 157 us (0.987)
    pallas_call x1, Pallas kernels: 152 us -> 150 us  [local_head(): pl.pallas_call(functools.partial(head_kernel, vocab, tile), out_shape=(ja...]
where the time goes in v7:
time: 157 us
  Pallas kernels  155 us (99%)
  between operations  2.41 us (2%)
    pallas_call x1, Pallas kernels, local_head(): pl.pallas_call(functools.partial(head_kernel, vocab, tile), out_shape=(ja...  150 us
    pallas_call x1, Pallas kernels, local_head(): pl.pallas_call(functools.partial(finish_kernel, scale), out_shape=(jax.Sh...  4.61 us

profile of v7, /device:TPU:0, one launch (start us, length us, event | category | flops | bytes accessed | tf_op | source)
XLA Modules:
  0.0 157.1 jit_solution(248788721479685157)
XLA Ops:
  0.6 150.0 %shard_map.58 = (f32[1,128]{1,0:T(1,128)}, f32[4,512,128]{2,1,0:T(8,128)}, f32[2008,512]{1,0:T(8,128)}) custom-call(bf16[512,512]{1,0:T(8,128)(2,1)} %h_ref.1, s32[1,512]{1,0:T(1,128)} %bitcast.3, bf16[2008,512]{1,0:T(8,128)(2,1)} %w_ref.1), custom_call_target="tpu_custom_call" | custom-call | tf_op jit(solution)/shard_map/pallas_call | solution.py:411
  151.3 4.6 %shard_map.59 = (f32[512,512]{1,0:T(8,128)}, f32[2008,512]{1,0:T(8,128)}) custom-call(f32[4,512,128]{2,1,0:T(8,128)} %get-tuple-element.9.dht_ref, f32[2008,512]{1,0:T(8,128)} %get-tuple-element.10.dw_ref), custom_call_target="tpu_custom_call" | custom-call | tf_op jit(solution)/shard_map/pallas_call | solution.py:429
